TPU v7x, 32 devices: a whole 2x2x4 slice. The times are simulated.
32 devices in a mesh: beam: 4 (over y, x), row: 4 (over z), col: 2 (over core).
Axes of the slice: x: 2, y: 2, z: 4, core: 2. Of those that a mesh axis runs over, the one named last changes fastest.
Arguments:
- phase_volume: bfloat16 [64, 1024, 256], P('beam', 'row', 'col'), may hold values from -0.75 to 0.75
- absorb_volume: bfloat16 [64, 1024, 256], P('beam', 'row', 'col'), may hold values from -0.375 to 0.375
- probe: float32 [2, 256, 256], replicated, may hold values from -6 to 6
- amplitudes: bfloat16 [4, 2, 32, 256, 256], P('row', 'col', 'beam'), may hold values from 0.19921875 to 2.5
- scan_rows: int32 [4, 2, 32], P('row', 'col', 'beam'), may hold values from 0 to 255
- scan_cols: int32 [4, 2, 32], P('row', 'col', 'beam'), may hold values from 0 to 127
Outputs:
- object_step: float32 [2, 1024, 256], P(None, 'row', 'col')
- probe_gradient: float32 [2, 256, 256], replicated
- loss: float32 [], replicated
All inputs are finite; a program needn't handle non-finite values.
Results may differ from a plain program's by a relative error of at most 0.00055.
The roundings to bfloat16 on the way count: a program that leaves them out, or rounds other values in their place, can miss the bound.
Values sent between devices are 32-bit elements; how exact they have to be, the bound alone decides.
A program may use at most 64 MiB of HBM per device.

v0:
```python
import functools
import math

import jax
import jax.numpy as jnp
import numpy as np
from jax import lax
from jax.experimental import pallas as pl
from jax.experimental.pallas import tpu as pltpu
from jax.sharding import PartitionSpec as P


def dft_matrices(length):
    indices = np.arange(length, dtype=np.int32)
    product = indices[:, None] * indices[None, :] % length
    angles = product.astype(np.float32) * np.float32(2.0 * math.pi / length)
    factor = np.float32(1.0 / math.sqrt(length))
    real = (np.cos(angles) * factor).astype(jnp.bfloat16)
    imag = (-np.sin(angles) * factor).astype(jnp.bfloat16)
    left = np.block([[real, -imag], [imag, real]])
    right = np.block([[real, imag], [-imag, real]])
    return jnp.asarray(left), jnp.asarray(right)


def window_kernel(
    rows_ref, cols_ref, trans_ref, probe_ref, amplitude_ref, left_ref, right_ref,
    canvas_ref, term_ref, misfit_ref, kept,
):
    step = pl.program_id(0)
    pair = amplitude_ref.shape[0]
    length = probe_ref.shape[1]
    wide = trans_ref.shape[2]
    dot = functools.partial(jnp.dot, preferred_element_type=jnp.float32)

    @pl.when(step == 0)
    def _():
        canvas_ref[...] = jnp.zeros_like(canvas_ref)
        term_ref[...] = jnp.zeros_like(term_ref)
        misfit_ref[...] = jnp.zeros_like(misfit_ref)

    def place(which):
        row_at = rows_ref[step * pair + which]
        col_at = cols_ref[step * pair + which]
        return pl.multiple_of(row_at // 8 * 8, 8), row_at % 8, col_at

    def wave(which):
        trans_real, trans_imag = kept[which, 0], kept[which, 1]
        wave_real = probe_ref[0] * trans_real - probe_ref[1] * trans_imag
        wave_imag = probe_ref[0] * trans_imag + probe_ref[1] * trans_real
        return trans_real, trans_imag, wave_real, wave_imag

    def enter(which):
        row_base, row_rest, col_at = place(which)
        for part in range(2):
            rows = trans_ref[part, pl.ds(row_base, length + 8), :]
            rows = pltpu.roll(rows, length + 8 - row_rest, 0)[:length]
            kept[which, part] = pltpu.roll(rows, lax.rem(wide - col_at, wide), 1)[:, :length]
        _, _, wave_real, wave_imag = wave(which)
        return jnp.concatenate([wave_real, wave_imag], axis=0).astype(jnp.bfloat16)

    def transform(first, second, values):
        part = dot(first[...], values).astype(jnp.bfloat16)
        return dot(jnp.concatenate([part[:length], part[length:]], axis=1), second[...])

    def compare(which, far):
        far_real = far[:, :length]
        far_imag = far[:, length:]
        amplitude = amplitude_ref[which].astype(jnp.float32)
        modulus = jnp.sqrt(far_real * far_real + far_imag * far_imag)
        off = modulus - amplitude
        misfit_ref[...] += jnp.sum((off * off).reshape(length // 8, 8, length), axis=0)
        ratio = 1.0 - amplitude / jnp.maximum(modulus, 0.5)
        residual = jnp.concatenate([far_real * ratio, far_imag * ratio], axis=0)
        return residual.astype(jnp.bfloat16)

    def leave(which, near):
        row_base, row_rest, col_at = place(which)
        grad_real = near[:, :length]
        grad_imag = near[:, length:]
        trans_real, trans_imag, wave_real, wave_imag = wave(which)
        term_ref[0] += trans_real * grad_real + trans_imag * grad_imag
        term_ref[1] += trans_real * grad_imag - trans_imag * grad_real
        side = jnp.zeros((length, wide - length), jnp.float32)
        below = jnp.zeros((8, wide), jnp.float32)
        object_terms = (
            wave_real * grad_imag - wave_imag * grad_real,
            -(wave_real * grad_real + wave_imag * grad_imag),
        )
        for part, values in enumerate(object_terms):
            placed = pltpu.roll(jnp.concatenate([values, side], axis=1), col_at, 1)
            placed = pltpu.roll(jnp.concatenate([placed, below], axis=0), row_rest, 0)
            canvas_ref[part, pl.ds(row_base, length + 8), :] += placed

    waves = [enter(which) for which in range(pair)]
    fars = [transform(left_ref, right_ref, wave_now) for wave_now in waves]
    residuals = [compare(which, fars[which]) for which in range(pair)]
    nears = [transform(right_ref, left_ref, residual) for residual in residuals]
    for which in range(pair):
        leave(which, nears[which])


def window_terms(trans, probe, amplitude, rows, cols):
    count, length = amplitude.shape[:2]
    pair = 2 if count % 2 == 0 else 1
    left, right = dft_matrices(length)
    whole = lambda array: pl.BlockSpec(array.shape, lambda s, r, c: (0,) * array.ndim)
    outs = [
        jax.ShapeDtypeStruct(trans.shape, jnp.float32),
        jax.ShapeDtypeStruct(probe.shape, jnp.float32),
        jax.ShapeDtypeStruct((8, length), jnp.float32),
    ]
    return pl.pallas_call(
        window_kernel,
        out_shape=outs,
        grid_spec=pltpu.PrefetchScalarGridSpec(
            num_scalar_prefetch=2,
            grid=(count // pair,),
            in_specs=[
                whole(trans),
                whole(probe),
                pl.BlockSpec((pair, length, length), lambda s, r, c: (s, 0, 0)),
                whole(left),
                whole(right),
            ],
            out_specs=[whole(out) for out in outs],
            scratch_shapes=[pltpu.VMEM((pair, 2, length, length), jnp.float32)],
        ),
        compiler_params=pltpu.CompilerParams(
            dimension_semantics=("arbitrary",), vmem_limit_bytes=48 * 2**20
        ),
    )(rows, cols, trans, probe, amplitude, left, right)


class Sends:
    def __init__(self, axes, send_sem, recv_sem):
        self.axes, self.sends, self.recvs, self.used = axes, send_sem, recv_sem, 0

    def greet(self):
        barrier = pltpu.get_barrier_semaphore()
        peers = 0
        for axis, (me, count) in self.axes.items():
            for d in range(1, count):
                pl.semaphore_signal(
                    barrier, inc=1, device_id={axis: lax.rem(me + d, count)},
                    device_id_type=pl.DeviceIdType.MESH,
                )
                peers += 1
        pl.semaphore_wait(barrier, peers)

    def copy(self, axis, peer, src, dst):
        index = self.used
        self.used += 1
        return pltpu.make_async_remote_copy(
            src_ref=src, dst_ref=dst, send_sem=self.sends.at[index],
            recv_sem=self.recvs.at[index], device_id={axis: peer},
            device_id_type=pl.DeviceIdType.MESH,
        )

    def each(self, axis, source, target):
        me, count = self.axes[axis]
        copies = []
        for d in range(1, count):
            peer = lax.rem(me + d, count)
            one = self.copy(axis, peer, source(peer), target(d - 1))
            one.start()
            copies.append(one)
        return copies

    def sides(self, axis, down, up, to_before=True, to_after=True):
        me, count = self.axes[axis]
        before = self.copy(axis, lax.rem(me + count - 1, count), *down)
        after = self.copy(axis, lax.rem(me + 1, count), *up)
        has_before, has_after = me > 0, me < count - 1
        both = jnp.logical_and
        pl.when(both(has_before, to_before))(before.start)
        pl.when(both(has_after, to_after))(after.start)

        def finish():
            pl.when(both(has_before, to_before))(before.wait_send)
            pl.when(both(has_after, to_after))(after.wait_send)
            pl.when(both(has_after, to_before))(before.wait_recv)
            pl.when(both(has_before, to_after))(after.wait_recv)

        return finish


def wait_all(copies):
    for one in copies:
        one.wait()


def axes_of(sizes):
    return {axis: (lax.axis_index(axis), count) for axis, count in sizes}


def project_kernel(sizes, half, phase_ref, absorb_ref, out_ref, part, slots, strip, side, send_sem, recv_sem):
    axes = axes_of(sizes)
    net = Sends(axes, send_sem, recv_sem)
    beam, beams = axes["beam"]
    row, rows_count = axes["row"]
    col, cols_count = axes["col"]
    depth, rows, cols = phase_ref.shape
    share = rows // beams
    edge = half // share
    strip[0] = jnp.ones(strip.shape[1:], jnp.float32)
    strip[1] = jnp.zeros(strip.shape[1:], jnp.float32)
    side[:, 0] = jnp.ones((2,) + strip.shape[1:], jnp.float32)
    side[:, 1] = jnp.zeros((2,) + strip.shape[1:], jnp.float32)
    net.greet()
    for plane, ref in enumerate((phase_ref, absorb_ref)):
        total = ref[0].astype(jnp.float32)
        for d in range(1, depth):
            total += ref[d].astype(jnp.float32)
        part[:, plane] = total.reshape(beams, share, cols)
    scatter = net.each("beam", lambda peer: part.at[peer], lambda d: slots.at[d])
    wait_all(scatter)
    total = part[beam]
    for d in range(beams - 1):
        total += slots[d]
    damping = jnp.exp(-total[1])
    own = edge + beam
    strip[0, own] = damping * jnp.cos(total[0])
    strip[1, own] = damping * jnp.sin(total[0])
    gather = net.each("beam", lambda peer: strip.at[:, own], lambda d: strip.at[:, own])
    finishes = []
    for d in range(beams):
        if d:
            gather[d - 1].wait_recv()
        share_at = lax.rem(beam + beams - d, beams)
        here = strip.at[:, edge + share_at]
        finishes.append(net.sides(
            "row",
            (here, strip.at[:, lax.rem(edge + beams + share_at, strip.shape[1])]),
            (here, strip.at[:, lax.rem(edge + share_at + strip.shape[1] - beams, strip.shape[1])]),
            share_at < edge, share_at >= beams - edge,
        ))
    for one in gather:
        one.wait_send()
    for finish in finishes:
        finish()
    finish = net.sides("col", (strip, side.at[1]), (strip, side.at[0]))
    out_ref[:, :, half : half + cols] = strip[...].reshape(2, rows + 2 * half, cols)
    finish()
    out_ref[:, :, :half] = side[0].reshape(2, rows + 2 * half, cols)[:, :, cols - half :]
    out_ref[:, :, half + cols :] = side[1].reshape(2, rows + 2 * half, cols)[:, :, :half]


def comm_params(number):
    return pltpu.CompilerParams(
        collective_id=number, has_side_effects=True, vmem_limit_bytes=48 * 2**20
    )


def vmem_specs(count):
    return [pl.BlockSpec(memory_space=pltpu.VMEM)] * count


def project(sizes, half, phase_volume, absorb_volume):
    depth, rows, cols = phase_volume.shape
    beams = dict(sizes)["beam"]
    share = rows // beams
    f32 = jnp.float32
    wires = sum(count for _, count in sizes) * 2 + 2 * beams
    tall = rows + 2 * half
    return pl.pallas_call(
        functools.partial(project_kernel, sizes, half),
        out_shape=jax.ShapeDtypeStruct((2, tall, cols + 2 * half), f32),
        in_specs=vmem_specs(2),
        out_specs=vmem_specs(1)[0],
        scratch_shapes=[
            pltpu.VMEM((beams, 2, share, cols), f32),
            pltpu.VMEM((beams - 1, 2, share, cols), f32),
            pltpu.VMEM((2, tall // share, share, cols), f32),
            pltpu.VMEM((2, 2, tall // share, share, cols), f32),
            pltpu.SemaphoreType.DMA((wires,)),
            pltpu.SemaphoreType.DMA((wires,)),
        ],
        compiler_params=comm_params(1),
    )(phase_volume, absorb_volume)


def combine_kernel(
    sizes, half, entries, positions, canvas_ref, term_ref, misfit_ref,
    step_ref, probe_ref, loss_ref,
    left, right, side, strip, strip_in, folded, rims, mine, grads,
    term_col, term_a, term_beam, term_b, term_row, result, small, small_sum,
    send_sem, recv_sem,
):
    axes = axes_of(sizes)
    net = Sends(axes, send_sem, recv_sem)
    beam, beams = axes["beam"]
    row, rows_count = axes["row"]
    col, cols_count = axes["col"]
    blocks = strip.shape[1]
    cols = strip.shape[4]
    rims[...] = jnp.zeros_like(rims)
    net.greet()
    left[...] = canvas_ref[:, :, :half]
    right[...] = canvas_ref[:, :, half + cols :]
    finish = net.sides("col", (left, side.at[1]), (right, side.at[0]))
    term_copies = net.each("col", lambda peer: term_ref.at[peer], lambda d: term_col.at[d])
    side_zero = jnp.zeros(side.shape[1:], jnp.float32)

    @pl.when(col == 0)
    def _():
        side[0] = side_zero

    @pl.when(col == cols_count - 1)
    def _():
        side[1] = side_zero

    finish()
    folded_now = canvas_ref[:, :, half : half + cols]
    lower = folded_now[:, :, :half] + side[0]
    strip[...] = (lower + side[1]).reshape(strip.shape)
    finish = net.sides(
        "row",
        (strip.at[:, 0], rims.at[1]),
        (strip.at[:, blocks - 1], rims.at[0]),
    )
    wait_all(term_copies)
    total = term_ref[col]
    for d in range(cols_count - 1):
        total += term_col[d]
    term_a[...] = total
    term_copies = net.each("beam", lambda peer: term_a.at[peer], lambda d: term_beam.at[d])
    finish()
    folded[...] = strip[:, 1 : blocks - 1]
    folded[:, 0] += rims[0]
    folded[:, blocks - 3] += rims[1]
    grid_copies = net.each("beam", lambda peer: folded.at[:, :, peer], lambda d: strip_in.at[d])
    wait_all(term_copies)
    total = term_a[beam]
    for d in range(beams - 1):
        total += term_beam[d]
    term_b[...] = total
    term_copies = net.each("row", lambda peer: term_b.at[peer], lambda d: term_row.at[d])
    wait_all(grid_copies)
    total = folded[:, :, beam]
    for d in range(beams - 1):
        total += strip_in[d]
    mine[...] = total
    grad_copies = net.each("beam", lambda peer: mine, lambda d: grads.at[:, :, beam])
    values = mine[...]
    square = jnp.sum((values * values).reshape(-1, 8, cols), axis=0)
    misfit_sum = misfit_ref[:, :cols]
    for k in range(1, misfit_ref.shape[1] // cols):
        misfit_sum += misfit_ref[:, k * cols : (k + 1) * cols]
    small_sum[0, 0] = square
    small_sum[0, 1] = misfit_sum
    base = 0

    def share_small(axis, level, base):
        count = axes[axis][1]
        return net.each(axis, lambda peer: small_sum.at[level], lambda d: small.at[base + d]), base + count - 1

    def add_small(level, begin, end):
        total = small_sum[level]
        for k in range(begin, end):
            total += small[k]
        small_sum[level + 1] = total

    small_copies, first = share_small("row", 0, 0)
    wait_all(term_copies)
    total = term_b[row]
    for d in range(rows_count - 1):
        total += term_row[d]
    total = total * (1.0 / positions)
    result[col, beam, row] = total
    term_copies = net.each("row", lambda peer: result.at[col, beam, row], lambda d: result.at[col, beam, row])
    wait_all(small_copies)
    add_small(0, 0, first)
    small_copies, second = share_small("beam", 1, first)
    wait_all(term_copies)
    term_copies = net.each("beam", lambda peer: result.at[col, beam], lambda d: result.at[col, beam])
    wait_all(small_copies)
    add_small(1, first, second)
    small_copies, third = share_small("col", 2, second)
    wait_all(grad_copies)
    grads[:, :, beam] = mine[...]
    wait_all(small_copies)
    add_small(2, second, third)
    mean_square = jnp.sum(small_sum[3, 0], keepdims=True) / entries
    factor = jnp.minimum(1.0, 0.5 / jnp.sqrt(mean_square + 1e-06))
    step_ref[...] = grads[...] * factor[None, None, None]
    loss_ref[...] = jnp.broadcast_to(jnp.sum(small_sum[3, 1], keepdims=True), loss_ref.shape)
    wait_all(term_copies)
    term_copies = net.each("col", lambda peer: result.at[col], lambda d: result.at[col])
    wait_all(term_copies)
    probe_ref[...] = result[...]


def combine(sizes, half, rows, cols, positions, canvas, term, misfit):
    counts = dict(sizes)
    beams, rows_count, cols_count = counts["beam"], counts["row"], counts["col"]
    f32 = jnp.float32
    blocks = rows // half + 2
    thin = half // beams
    lines = term.shape[0] * term.shape[1] // (cols_count * beams * rows_count)
    width = term.shape[2]
    pieces = (cols_count, beams, rows_count, lines, width)
    entries = 2 * rows * cols * rows_count * cols_count
    wires = 4 * sum(counts.values())
    tall = canvas.shape[1]
    grid = (2, blocks - 2, beams, thin, cols)
    step, probe_gradient, loss = pl.pallas_call(
        functools.partial(combine_kernel, sizes, half, entries, positions),
        out_shape=[
            jax.ShapeDtypeStruct(grid, f32),
            jax.ShapeDtypeStruct(pieces, f32),
            jax.ShapeDtypeStruct((8, 128), f32),
        ],
        in_specs=vmem_specs(3),
        out_specs=vmem_specs(3),
        scratch_shapes=[
            pltpu.VMEM((2, tall, half), f32),
            pltpu.VMEM((2, tall, half), f32),
            pltpu.VMEM((2, 2, tall, half), f32),
            pltpu.VMEM((2, blocks, beams, thin, cols), f32),
            pltpu.VMEM((beams - 1, 2, blocks - 2, thin, cols), f32),
            pltpu.VMEM(grid, f32),
            pltpu.VMEM((2, 2, beams, thin, cols), f32),
            pltpu.VMEM((2, blocks - 2, thin, cols), f32),
            pltpu.VMEM(grid, f32),
            pltpu.VMEM((cols_count - 1,) + pieces[1:], f32),
            pltpu.VMEM(pieces[1:], f32),
            pltpu.VMEM((beams - 1,) + pieces[2:], f32),
            pltpu.VMEM(pieces[2:], f32),
            pltpu.VMEM((rows_count - 1,) + pieces[3:], f32),
            pltpu.VMEM(pieces, f32),
            pltpu.VMEM((sum(counts.values()), 2, 8, cols), f32),
            pltpu.VMEM((4, 2, 8, cols), f32),
            pltpu.SemaphoreType.DMA((wires,)),
            pltpu.SemaphoreType.DMA((wires,)),
        ],
        compiler_params=comm_params(2),
    )(canvas, term.reshape(pieces), misfit)
    return (
        step.reshape(2, rows, cols),
        probe_gradient.reshape(term.shape),
        loss[0, 0] / (positions * width * width),
    )


def local(phase_volume, absorb_volume, probe, amplitudes, scan_rows, scan_cols):
    length = probe.shape[1]
    half = length // 2
    count = scan_rows.shape[2]
    rows, cols = phase_volume.shape[1:]
    sizes = tuple((axis, lax.axis_size(axis)) for axis in ("beam", "row", "col"))
    trans = project(sizes, half, phase_volume, absorb_volume)
    canvas, term, misfit = window_terms(
        trans, probe, amplitudes.reshape(count, length, length),
        scan_rows.reshape(count), scan_cols.reshape(count),
    )
    positions = count * math.prod(size for _, size in sizes)
    return combine(sizes, half, rows, cols, positions, canvas, term, misfit)


def solution(mesh):
    in_specs = (
        P("beam", "row", "col"),
        P("beam", "row", "col"),
        P(),
        P("row", "col", "beam", None, None),
        P("row", "col", "beam"),
        P("row", "col", "beam"),
    )
    out_specs = (P(None, "row", "col"), P(), P())
    return jax.shard_map(local, mesh=mesh, in_specs=in_specs, out_specs=out_specs, check_vma=False)
```

profile of v0, /device:TPU:0, one launch (start us, length us, event | category | flops | bytes accessed | tf_op | source)
XLA Modules:
  0.0 67.6 jit_solution(7395018948970303858)
XLA Ops:
  0.6 0.0 copy-start.1
  0.6 1.2 %copy-done.1 = bf16[16,256,128]{2,1,0:T(8,128)(2,1)S(1)} copy-done((bf16[16,256,128]{2,1,0:T(8,128)(2,1)S(1)}, bf16[16,256,128]{2,1,0:T(8,128)(2,1)}, u32[]{:S(2)}) %copy-start.1) | copy-done | bytes 1048600
  1.9 0.0 copy-start.2
  1.9 1.2 %copy-done.2 = bf16[16,256,128]{2,1,0:T(8,128)(2,1)S(1)} copy-done((bf16[16,256,128]{2,1,0:T(8,128)(2,1)S(1)}, bf16[16,256,128]{2,1,0:T(8,128)(2,1)}, u32[]{:S(2)}) %copy-start.2) | copy-done | bytes 1048600
  3.1 0.0 copy-start.3
  3.1 0.0 copy-start.4
  3.1 0.0 copy-start.5
  3.1 0.0 copy-start.6
  3.1 0.0 copy-start.7
  3.1 0.0 copy-start.8
  3.1 19.7 %shard_map.103.trans_ref = f32[2,512,384]{2,1,0:T(8,128)S(1)} custom-call(bf16[16,256,128]{2,1,0:T(8,128)(2,1)S(1)} %copy-done.1, bf16[16,256,128]{2,1,0:T(8,128)(2,1)S(1)} %copy-done.2), custom_call_target="tpu_custom_call" | custom-call | tf_op jit(solution)/shard_map/pallas_call | solution.py:265
  22.9 0.0 copy-start
  22.9 1.1 %copy-done = f32[2,512,384]{2,1,0:T(8,128)} copy-done((f32[2,512,384]{2,1,0:T(8,128)}, f32[2,512,384]{2,1,0:T(8,128)S(1)}, u32[]{:S(2)}) %copy-start) | copy-done | bytes 1572888
  24.0 0.0 copy-done.3
  24.0 0.0 copy-done.4
  24.0 0.0 copy-done.5
  24.0 0.0 copy-done.6
  24.0 0.0 copy-done.7
  24.0 0.0 copy-done.8
  24.0 15.9 %shard_map.104 = (f32[2,512,384]{2,1,0:T(8,128)S(1)}, f32[2,256,256]{2,1,0:T(8,128)S(1)}, f32[8,256]{1,0:T(8,128)S(1)}) custom-call(s32[8]{0:T(128)S(1)} %bitcast.11, s32[8]{0:T(128)S(1)} %bitcast.12, f32[2,512,384]{2,1,0:T(8,128)} %copy-done, f32[2,256,256]{2,1,0:T(8,128)S(1)} %copy-done.4, bf16[8,256,256]{2,1,0:T(8,128)(2,1)S(1)} %bitcast.7, ...), custom_call_target="tpu_custom_call" | custom-call | tf_op jit(solution)/shard_map/pallas_call | solution.py:112
  39.9 23.9 %shard_map.105 = (f32[2,2,4,32,128]{4,3,2,1,0:T(8,128)S(1)}, f32[2,4,4,16,256]{4,3,2,1,0:T(8,128)S(1)}, f32[8,128]{1,0:T(8,128)S(1)}) custom-call(f32[2,512,384]{2,1,0:T(8,128)S(1)} %get-tuple-element.9.canvas_ref, f32[2,4,4,16,256]{4,3,2,1,0:T(8,128)S(1)} %bitcast.9, f32[8,256]{1,0:T(8,128)S(1)} %get-tuple-element.11.misfit_ref), custom_call_target="tpu_custom_call" | custom-call | tf_op jit(solution)/shard_map/pallas_call | solution.py:406
  63.8 0.5 slice.3
  65.0 0.7 %copy.13 = f32[2,256,128]{2,1,0:T(8,128)} copy(f32[2,256,128]{2,1,0:T(8,128)S(1)} %bitcast.10) | data formatting | bytes 524288
  65.7 0.8 %copy.14 = f32[2,256,256]{2,1,0:T(8,128)} copy(f32[2,256,256]{2,1,0:T(8,128)S(1)} %bitcast.8) | data formatting | bytes 1048576
Async XLA Ops:
  0.6 1.2 %copy-start.1 = (bf16[16,256,128]{2,1,0:T(8,128)(2,1)S(1)}, bf16[16,256,128]{2,1,0:T(8,128)(2,1)}, u32[]{:S(2)}) copy-start(bf16[16,256,128]{2,1,0:T(8,128)(2,1)} %phase_ref.1) | copy-start | bytes 3145732
  1.9 1.2 %copy-start.2 = (bf16[16,256,128]{2,1,0:T(8,128)(2,1)S(1)}, bf16[16,256,128]{2,1,0:T(8,128)(2,1)}, u32[]{:S(2)}) copy-start(bf16[16,256,128]{2,1,0:T(8,128)(2,1)} %absorb_ref.1) | copy-start | bytes 3145732
  3.1 20.9 %copy-start.3 = (bf16[1,1,8,256,256]{4,3,2,1,0:T(8,128)(2,1)S(1)}, bf16[1,1,8,256,256]{4,3,2,1,0:T(8,128)(2,1)}, u32[]{:S(2)}) copy-start(bf16[1,1,8,256,256]{4,3,2,1,0:T(8,128)(2,1)} %param.11) | copy-start | bytes 3145732
  3.1 20.9 %copy-start.4 = (f32[2,256,256]{2,1,0:T(8,128)S(1)}, f32[2,256,256]{2,1,0:T(8,128)}, u32[]{:S(2)}) copy-start(f32[2,256,256]{2,1,0:T(8,128)} %probe_ref.1) | copy-start | bytes 1572868
  3.1 20.9 %copy-start.5 = (bf16[512,512]{1,0:T(8,128)(2,1)S(1)}, bf16[512,512]{1,0:T(8,128)(2,1)}, u32[]{:S(2)}) copy-start(bf16[512,512]{1,0:T(8,128)(2,1)} %constant.9.clone.right_ref) | copy-start | bytes 1572868
  3.1 20.9 %copy-start.6 = (bf16[512,512]{1,0:T(8,128)(2,1)S(1)}, bf16[512,512]{1,0:T(8,128)(2,1)}, u32[]{:S(2)}) copy-start(bf16[512,512]{1,0:T(8,128)(2,1)} %constant.8.clone.left_ref) | copy-start | bytes 1572868
  3.1 20.9 %copy-start.7 = (s32[1,1,8]{2,1,0:T(1,128)S(1)}, s32[1,1,8]{2,1,0:T(1,128)}, u32[]{:S(2)}) copy-start(s32[1,1,8]{2,1,0:T(1,128)} %param.12) | copy-start | bytes 100
  3.1 20.9 %copy-start.8 = (s32[1,1,8]{2,1,0:T(1,128)S(1)}, s32[1,1,8]{2,1,0:T(1,128)}, u32[]{:S(2)}) copy-start(s32[1,1,8]{2,1,0:T(1,128)} %param.13) | copy-start | bytes 100
  22.9 1.2 %copy-start = (f32[2,512,384]{2,1,0:T(8,128)}, f32[2,512,384]{2,1,0:T(8,128)S(1)}, u32[]{:S(2)}) copy-start(f32[2,512,384]{2,1,0:T(8,128)S(1)} %shard_map.103.trans_ref) | copy-start | bytes 4718596
where the time goes:
time: 67.9 us; the launch traced here: 67.6 us
  Pallas kernels  59.5 us (88%)
  local copies, waits for them, and re-layouts  5.62 us (8%)
  between operations  2.5 us (4%)
    pallas_call x1, Pallas kernels, combine(): pl.pallas_call(functools.partial(combine_kernel, sizes, half, entries, po...  23.9 us
    pallas_call x1, Pallas kernels, project(): pl.pallas_call(functools.partial(project_kernel, sizes, half), out_shape=...  19.7 us
    pallas_call x1, Pallas kernels, window_terms(): pl.pallas_call(window_kernel, out_shape=outs, grid_spec=pltpu.PrefetchSca...  15.9 us
    unnamed x20, local copies, waits for them, and re-layouts  5.11 us

commit v1 on v0

v1 whole, which is shorter than its diff:
```python
import functools
import math

import jax
import jax.numpy as jnp
import numpy as np
from jax import lax
from jax.experimental import pallas as pl
from jax.experimental.pallas import tpu as pltpu
from jax.sharding import PartitionSpec as P


def dft_matrices(length):
    indices = np.arange(length, dtype=np.int32)
    product = indices[:, None] * indices[None, :] % length
    angles = product.astype(np.float32) * np.float32(2.0 * math.pi / length)
    factor = np.float32(1.0 / math.sqrt(length))
    real = (np.cos(angles) * factor).astype(jnp.bfloat16)
    imag = (-np.sin(angles) * factor).astype(jnp.bfloat16)
    left = np.block([[real, -imag], [imag, real]])
    right = np.block([[real, imag], [-imag, real]])
    return jnp.asarray(left), jnp.asarray(right)


def window_kernel(
    rows_ref, cols_ref, trans_ref, probe_ref, amplitude_ref, left_ref, right_ref,
    canvas_ref, term_ref, misfit_ref, kept, wave, half, chi, back,
):
    count, length = amplitude_ref.shape[:2]
    lanes = trans_ref.shape[3]
    blocks = trans_ref.shape[1]
    inner = length // lanes
    step = 32
    steps = length // step
    dot = functools.partial(jnp.dot, preferred_element_type=jnp.float32)
    canvas_ref[...] = jnp.zeros_like(canvas_ref)
    term_ref[...] = jnp.zeros_like(term_ref)
    misfit_ref[...] = jnp.zeros_like(misfit_ref)
    lane = lax.broadcasted_iota(jnp.int32, (step, lanes), 1)

    def enter(w, slot, m):
        row_at, col_at = rows_ref[w], cols_ref[w]
        shift = lax.rem(lanes - col_at, lanes)
        keep = lane < lanes - col_at
        here = pl.ds(m * step, step)
        planes = []
        for part in range(2):
            turned = [
                pltpu.roll(trans_ref[part, k, pl.ds(row_at + m * step, step), :], shift, 1)
                for k in range(blocks)
            ]
            planes.append([jnp.where(keep, turned[k], turned[k + 1]) for k in range(inner)])
        for k in range(inner):
            real, imag = planes[0][k], planes[1][k]
            at = pl.ds(k * lanes, lanes)
            probe_real, probe_imag = probe_ref[0, here, at], probe_ref[1, here, at]
            kept[slot, 0, here, at] = real
            kept[slot, 1, here, at] = imag
            wave[slot, pl.ds(m * step, step), at] = (probe_real * real - probe_imag * imag).astype(jnp.bfloat16)
            wave[slot, pl.ds(length + m * step, step), at] = (probe_real * imag + probe_imag * real).astype(jnp.bfloat16)

    def compare(w, slot, m, far):
        rows = far.shape[0]
        here = pl.ds(m, rows)
        real, imag = far[:, :length], far[:, length:]
        amplitude = amplitude_ref[w, here, :].astype(jnp.float32)
        square = real * real + imag * imag
        inverse = lax.rsqrt(jnp.maximum(square, 1.2e-38))
        off = square * inverse - amplitude
        misfit_ref[...] += jnp.sum((off * off).reshape(rows // 8, 8, length), axis=0)
        ratio = 1.0 - amplitude * jnp.minimum(inverse, 2.0)
        chi[slot, here, :] = (real * ratio).astype(jnp.bfloat16)
        chi[slot, pl.ds(length + m, rows), :] = (imag * ratio).astype(jnp.bfloat16)

    def leave(w, slot, m, grad):
        rows = grad.shape[0]
        row_at, col_at = rows_ref[w], cols_ref[w]
        here = pl.ds(m, rows)
        lane = lax.broadcasted_iota(jnp.int32, (rows, lanes), 1)
        first = lane >= col_at
        objects = [[], []]
        for k in range(inner):
            at = pl.ds(k * lanes, lanes)
            grad_real = grad[:, k * lanes : (k + 1) * lanes]
            grad_imag = grad[:, length + k * lanes : length + (k + 1) * lanes]
            real, imag = kept[slot, 0, here, at], kept[slot, 1, here, at]
            term_real = real * grad_real + imag * grad_imag
            term_imag = real * grad_imag - imag * grad_real
            term_ref[0, here, at] += term_real
            term_ref[1, here, at] += term_imag
            probe_real, probe_imag = probe_ref[0, here, at], probe_ref[1, here, at]
            objects[0].append(pltpu.roll(probe_real * term_imag - probe_imag * term_real, col_at, 1))
            objects[1].append(pltpu.roll(probe_real * term_real + probe_imag * term_imag, col_at, 1))
        there = pl.ds(row_at + m, rows)
        for part in range(2):
            turned = objects[part]
            for k in range(blocks):
                before = turned[k - 1] if k > 0 else 0.0
                after = turned[k] if k < inner else 0.0
                value = jnp.where(first, after, before)
                if part:
                    canvas_ref[part, k, there, :] -= value
                else:
                    canvas_ref[part, k, there, :] += value

    def left(values, first, out, slot):
        part = dot(first[...], values[slot])
        out[slot, :, :length] = part[:length].astype(jnp.bfloat16)
        out[slot, :, length:] = part[length:].astype(jnp.bfloat16)

    def far_of(w, slot):
        far = dot(half[slot], right_ref[...])
        return [functools.partial(compare, w, slot, m * step, far[m * step : (m + 1) * step]) for m in range(steps)]

    def near_of(w, slot):
        near = dot(back[slot], left_ref[...])
        return [functools.partial(leave, w, slot, m * step, near[m * step : (m + 1) * step]) for m in range(steps)]

    def run(parts):
        for part in parts:
            part()

    def enters(w):
        return [functools.partial(enter, w, w % 2, m) for m in range(steps)] if w < count else []

    def halves(make, source, table, w, slot, cut):
        tall = length // cut
        for c in range(cut):
            out = dot(source[slot, c * tall : (c + 1) * tall], table[...])
            for m in range(tall // step):
                make(w, slot, c * tall + m * step, out[m * step : (m + 1) * step])

    run(enters(0))
    for p in range(count // 2):
        a, b = 2 * p, 2 * p + 1
        left(wave, left_ref, half, 0)
        if p:
            halves(leave, back, left_ref, b - 2, 1, 2)
        run(enters(b))
        left(wave, left_ref, half, 1)
        halves(compare, half, right_ref, a, 0, 2)
        left(chi, right_ref, back, 0)
        halves(compare, half, right_ref, b, 1, 2)
        left(chi, right_ref, back, 1)
        halves(leave, back, left_ref, a, 0, 2)
        run(enters(a + 2))
    halves(leave, back, left_ref, count - 1, 1, 2)


def window_terms(trans, probe, amplitude, rows, cols):
    count, length = amplitude.shape[:2]
    left, right = dft_matrices(length)
    f32, bf16 = jnp.float32, jnp.bfloat16
    smem = pl.BlockSpec(memory_space=pltpu.SMEM)
    return pl.pallas_call(
        window_kernel,
        out_shape=[
            jax.ShapeDtypeStruct(trans.shape, f32),
            jax.ShapeDtypeStruct(probe.shape, f32),
            jax.ShapeDtypeStruct((8, length), f32),
        ],
        in_specs=[smem, smem] + vmem_specs(5),
        out_specs=vmem_specs(3),
        scratch_shapes=[
            pltpu.VMEM((2, 2, length, length), f32),
            pltpu.VMEM((2, 2 * length, length), bf16),
            pltpu.VMEM((2, length, 2 * length), bf16),
            pltpu.VMEM((2, 2 * length, length), bf16),
            pltpu.VMEM((2, length, 2 * length), bf16),
        ],
        compiler_params=pltpu.CompilerParams(vmem_limit_bytes=40 * 2**20),
    )(rows, cols, trans, probe, amplitude, left, right)


def partners(me, count):
    if count % 4 == 0:
        high, low = me // 4 * 4 + me % 4 // 2 * 2, me % 2
        flips = [(1, 1), (0, 1), (1, 0)]
        near = []
        for up, across in flips:
            other = me // 4 * 4 + lax.rem(me % 4 // 2 + up, 2) * 2 + lax.rem(low + across, 2)
            near.append(other)
        if count == 4:
            return near
    return [lax.rem(me + d, count) for d in range(1, count)]


class Sends:
    def __init__(self, sizes, send_sem, recv_sem):
        self.axes = {axis: (lax.axis_index(axis), count) for axis, count in sizes}
        self.sends, self.recvs, self.used = send_sem, recv_sem, 0
        self.started = []

    def greet(self, groups):
        barrier = pltpu.get_barrier_semaphore()
        for target in groups:
            pl.semaphore_signal(barrier, inc=1, device_id=target, device_id_type=pl.DeviceIdType.MESH)
        pl.semaphore_wait(barrier, len(groups))

    def others(self, axis):
        return partners(*self.axes[axis])

    def copy(self, target, src, dst):
        index = self.used
        self.used += 1
        return pltpu.make_async_remote_copy(
            src_ref=src, dst_ref=dst, send_sem=self.sends.at[index],
            recv_sem=self.recvs.at[index], device_id=target,
            device_id_type=pl.DeviceIdType.MESH,
        )

    def send(self, target, src, dst):
        one = self.copy(target, src, dst)
        one.start()
        self.started.append(one.wait_send)
        return one

    def sides(self, axis, down, up, to_before=True, to_after=True):
        me, count = self.axes[axis]
        both = jnp.logical_and
        sends_before, sends_after = both(me > 0, to_before), both(me < count - 1, to_after)
        gets_after, gets_before = both(me < count - 1, to_before), both(me > 0, to_after)
        before = self.copy({axis: lax.rem(me + count - 1, count)}, *down)
        after = self.copy({axis: lax.rem(me + 1, count)}, *up)
        pl.when(sends_before)(before.start)
        pl.when(sends_after)(after.start)

        def wait_send():
            pl.when(sends_before)(before.wait_send)
            pl.when(sends_after)(after.wait_send)

        def wait_recv():
            pl.when(gets_after)(before.wait_recv)
            pl.when(gets_before)(after.wait_recv)

        self.started.append(wait_send)
        return wait_recv

    def finish(self):
        for wait_send in self.started:
            wait_send()


def project_kernel(sizes, half, phase_ref, absorb_ref, out_ref, volume, part, slots, load_sem, send_sem, recv_sem):
    net = Sends(sizes, send_sem, recv_sem)
    beam, beams = net.axes["beam"]
    depth, rows, cols = phase_ref.shape
    share = rows // beams
    edge = half // share
    blocks = out_ref.shape[2]
    peers = net.others("beam")
    order = peers + [beam]
    loads = []
    for i, peer in enumerate(order):
        here = pl.ds(pl.multiple_of(peer * share, share), share)
        for plane, ref in enumerate((phase_ref, absorb_ref)):
            one = pltpu.make_async_copy(ref.at[:, here, :], volume.at[plane, i], load_sem.at[plane, i])
            one.start()
            loads.append(one)
    out_ref[0] = jnp.ones(out_ref.shape[1:], jnp.float32)
    out_ref[1] = jnp.zeros(out_ref.shape[1:], jnp.float32)
    targets = [{axis: peer} for axis in net.axes for peer in net.others(axis)]
    net.greet(targets)
    scatter = []
    for i, peer in enumerate(order):
        for plane in range(2):
            loads[2 * i + plane].wait()
            total = volume[plane, i, 0].astype(jnp.float32)
            for d in range(1, depth):
                total += volume[plane, i, d].astype(jnp.float32)
            part[i, plane] = total
        if i < beams - 1:
            scatter.append(net.send({"beam": peer}, part.at[i], slots.at[i]))
    total = part[beams - 1]
    for i, one in enumerate(scatter):
        one.wait_recv()
        total += slots[i]
    damping = jnp.exp(-total[1])
    own = edge + beam
    out_ref[0, 1, own] = damping * jnp.cos(total[0])
    out_ref[1, 1, own] = damping * jnp.sin(total[0])
    at = lambda side, block: out_ref.at[:, side, block]
    arrivals = []

    def across(block, when=True):
        arrivals.append(net.sides("col", (at(1, block), at(2, block)), (at(1, block), at(0, block)), when, when))

    def along(share_at):
        here = at(1, edge + share_at)
        below = lax.rem(edge + beams + share_at, blocks)
        above = lax.rem(edge + share_at + blocks - beams, blocks)
        wait = net.sides(
            "row", (here, at(1, below)), (here, at(1, above)), share_at < edge, share_at >= beams - edge
        )
        return wait, share_at, below, above

    row, rows_count = net.axes["row"]
    gather = [net.send({"beam": peer}, at(1, own), at(1, own)) for peer in peers]
    rims = [along(beam)]
    across(own)
    for peer, one in zip(peers, gather):
        one.wait_recv()
        rims.append(along(peer))
        across(edge + peer)
    for wait, share_at, below, above in rims:
        wait()
        across(below, jnp.logical_and(row < rows_count - 1, share_at < edge))
        across(above, jnp.logical_and(row > 0, share_at >= beams - edge))
    for wait in arrivals:
        wait()
    net.finish()


def comm_params(number):
    return pltpu.CompilerParams(
        collective_id=number, has_side_effects=True, vmem_limit_bytes=40 * 2**20
    )


def vmem_specs(count):
    return [pl.BlockSpec(memory_space=pltpu.VMEM)] * count


def project(sizes, half, phase_volume, absorb_volume):
    depth, rows, cols = phase_volume.shape
    assert half == cols
    beams = dict(sizes)["beam"]
    share = rows // beams
    f32 = jnp.float32
    tall = rows + 2 * half
    wires = 2 * beams + 2 * beams + 6 * beams
    trans = pl.pallas_call(
        functools.partial(project_kernel, sizes, half),
        out_shape=jax.ShapeDtypeStruct((2, 3, tall // share, share, cols), f32),
        in_specs=[pl.BlockSpec(memory_space=pltpu.HBM)] * 2,
        out_specs=vmem_specs(1)[0],
        scratch_shapes=[
            pltpu.VMEM((2, beams, depth, share, cols), phase_volume.dtype),
            pltpu.VMEM((beams, 2, share, cols), f32),
            pltpu.VMEM((beams - 1, 2, share, cols), f32),
            pltpu.SemaphoreType.DMA((2, beams)),
            pltpu.SemaphoreType.DMA((wires,)),
            pltpu.SemaphoreType.DMA((wires,)),
        ],
        compiler_params=comm_params(1),
    )(phase_volume, absorb_volume)
    return trans.reshape(2, 3, tall, cols)


def combine_kernel(
    sizes, half, entries, positions, canvas_ref, term_ref, misfit_ref,
    grad_ref, probe_ref, scalar_ref,
    side, strip, rims, folded, folded_in,
    term_col, term_a, term_beam, term_b, term_row, small, small_col,
    send_sem, recv_sem,
):
    net = Sends(sizes, send_sem, recv_sem)
    beam, beams = net.axes["beam"]
    row, rows_count = net.axes["row"]
    col, cols_count = net.axes["col"]
    blocks = strip.shape[1]
    cols = strip.shape[4]
    beam_peers, row_peers, col_peers = (net.others(axis) for axis in ("beam", "row", "col"))
    order = beam_peers + [beam]
    row_order = row_peers + [row]
    wide = [{"beam": b, "row": r} for b in order for r in row_order][:-1]
    rims[...] = jnp.zeros_like(rims)

    @pl.when(col == 0)
    def _():
        side[0] = jnp.zeros(side.shape[1:], jnp.float32)

    @pl.when(col == cols_count - 1)
    def _():
        side[1] = jnp.zeros(side.shape[1:], jnp.float32)

    net.greet(wide + [{"col": c} for c in col_peers])

    across, term_across = [], []
    for p in order:
        term_across.append([
            net.send({"col": c}, term_ref.at[c, p], term_col.at[k, p]) for k, c in enumerate(col_peers)
        ])
        across.append(net.sides(
            "col",
            (canvas_ref.at[:, 0, :, p], side.at[1, :, :, p]),
            (canvas_ref.at[:, 2, :, p], side.at[0, :, :, p]),
        ))
    along, term_beams = [], []
    for i, p in enumerate(order):
        for one in term_across[i]:
            one.wait_recv()
        total = term_ref[col, p]
        for k in range(cols_count - 1):
            total += term_col[k, p]
        term_a[i] = total
        if i < beams - 1:
            term_beams.append([
                net.send({"beam": p}, term_a.at[i, r], term_beam.at[i, r]) for r in row_order
            ])
        across[i]()
        strip[:, :, p] = canvas_ref[:, 1, :, p] + side[0, :, :, p] + side[1, :, :, p]
        along.append(net.sides(
            "row",
            (strip.at[:, 0, p], rims.at[1, :, p]),
            (strip.at[:, blocks - 1, p], rims.at[0, :, p]),
        ))

    grids = []
    for i, p in enumerate(order):
        along[i]()
        middle = strip[:, 1 : blocks - 1, p]
        folded[i] = middle
        folded[i, :, 0] += rims[0, :, p]
        folded[i, :, blocks - 3] += rims[1, :, p]
        if i < beams - 1:
            grids.append(net.send({"beam": p}, folded.at[i], folded_in.at[i]))
    term_rows = []
    for k, r in enumerate(row_order):
        total = term_a[beams - 1, r]
        for i in range(beams - 1):
            term_beams[i][k].wait_recv()
            total += term_beam[i, r]
        term_b[k] = total
        if k < rows_count - 1:
            term_rows.append(net.send({"row": r}, term_b.at[k], term_row.at[k]))

    total = folded[beams - 1]
    for i, one in enumerate(grids):
        one.wait_recv()
        total += folded_in[i]
    grad_ref[:, :, beam] = total
    misfit_sum = misfit_ref[:, :cols]
    for k in range(1, misfit_ref.shape[1] // cols):
        misfit_sum += misfit_ref[:, k * cols : (k + 1) * cols]
    small[beam, row, 0] = jnp.sum((total * total).reshape(-1, 8, cols), axis=0)
    small[beam, row, 1] = misfit_sum
    smalls = [net.send(target, small.at[beam, row], small.at[beam, row]) for target in wide]
    mine = grad_ref.at[:, :, beam]
    grads = [net.send({"beam": p}, mine, mine) for p in beam_peers]

    total = term_b[rows_count - 1]
    for k, one in enumerate(term_rows):
        one.wait_recv()
        total += term_row[k]
    probe_ref[col, beam, row] = total * (1.0 / positions)
    piece = lambda b, r: probe_ref.at[col, b, r]
    row_copies = [net.send({"row": r}, piece(beam, row), piece(beam, row)) for r in row_peers]
    beam_copies = [[net.send({"beam": p}, piece(beam, row), piece(beam, row)) for p in beam_peers]]
    for one, r in zip(row_copies, row_peers):
        one.wait_recv()
        beam_copies.append([net.send({"beam": p}, piece(beam, r), piece(beam, r)) for p in beam_peers])
    col_copies = [net.send({"col": c}, probe_ref.at[col, beam], probe_ref.at[col, beam]) for c in col_peers]

    for one in smalls:
        one.wait_recv()
    total = small[0, 0]
    for k in range(1, beams * rows_count):
        total += small[k // rows_count, k % rows_count]
    small_col[col] = total
    small_copies = [net.send({"col": c}, small_col.at[col], small_col.at[col]) for c in col_peers]

    for i, p in enumerate(beam_peers):
        for group in beam_copies:
            group[i].wait_recv()
        col_copies += [net.send({"col": c}, probe_ref.at[col, p], probe_ref.at[col, p]) for c in col_peers]
    for one in small_copies:
        one.wait_recv()
    total = small_col[0]
    for k in range(1, cols_count):
        total += small_col[k]
    mean_square = jnp.sum(total[0], keepdims=True) / entries
    factor = jnp.minimum(1.0, 0.5 / jnp.sqrt(mean_square + 1e-06))
    scalar_ref[0] = jnp.broadcast_to(factor, scalar_ref.shape[1:])
    scalar_ref[1] = jnp.broadcast_to(jnp.sum(total[1], keepdims=True), scalar_ref.shape[1:])
    for one in grads + col_copies:
        one.wait_recv()
    net.finish()


def close_kernel(scale, grad_ref, probe_ref, scalar_ref, step_ref, gradient_ref, loss_ref, step, loss, sems):
    first = pltpu.make_async_copy(probe_ref, gradient_ref, sems.at[0])
    first.start()
    factor = scalar_ref[0, :1, :1]
    step[...] = grad_ref[...] * factor[None, None, None]
    second = pltpu.make_async_copy(step, step_ref, sems.at[1])
    second.start()
    loss[...] = scalar_ref[1, :1, :1] * scale
    third = pltpu.make_async_copy(loss, loss_ref, sems.at[2])
    third.start()
    first.wait()
    second.wait()
    third.wait()


def combine(sizes, half, rows, cols, positions, canvas, term, misfit):
    counts = dict(sizes)
    beams, rows_count, cols_count = counts["beam"], counts["row"], counts["col"]
    f32 = jnp.float32
    blocks = rows // half + 2
    thin = half // beams
    lines = term.shape[0] * term.shape[1] // (cols_count * beams * rows_count)
    width = term.shape[2]
    pieces = (cols_count, beams, rows_count, lines, width)
    entries = 2 * rows * cols * rows_count * cols_count
    wires = (
        (cols_count - 1) * 2 * beams + 5 * beams + (beams - 1) * 2 * rows_count
        + 2 * (rows_count - 1) + 2 * (beams - 1) + beams * rows_count + cols_count
    )
    grid = (2, blocks - 2, beams, thin, cols)
    shape = jax.ShapeDtypeStruct
    grad, probe_gradient, scalars = pl.pallas_call(
        functools.partial(combine_kernel, sizes, half, entries, positions),
        out_shape=[shape(grid, f32), shape(pieces, f32), shape((2, 8, 128), f32)],
        in_specs=vmem_specs(3),
        out_specs=vmem_specs(3),
        scratch_shapes=[
            pltpu.VMEM((2, 2, blocks, beams, thin, cols), f32),
            pltpu.VMEM((2, blocks, beams, thin, cols), f32),
            pltpu.VMEM((2, 2, beams, thin, cols), f32),
            pltpu.VMEM((beams, 2, blocks - 2, thin, cols), f32),
            pltpu.VMEM((beams - 1, 2, blocks - 2, thin, cols), f32),
            pltpu.VMEM((cols_count - 1,) + pieces[1:], f32),
            pltpu.VMEM(pieces[1:], f32),
            pltpu.VMEM((beams - 1,) + pieces[2:], f32),
            pltpu.VMEM(pieces[2:], f32),
            pltpu.VMEM((rows_count - 1,) + pieces[3:], f32),
            pltpu.VMEM((beams, rows_count, 2, 8, cols), f32),
            pltpu.VMEM((cols_count, 2, 8, cols), f32),
            pltpu.SemaphoreType.DMA((wires,)),
            pltpu.SemaphoreType.DMA((wires,)),
        ],
        compiler_params=comm_params(2),
    )(canvas.reshape(2, 3, blocks, beams, thin, cols), term.reshape(pieces), misfit)
    probe_gradient = probe_gradient.reshape(term.shape)
    anywhere = pl.BlockSpec(memory_space=pltpu.HBM)
    step, probe_gradient, loss = pl.pallas_call(
        functools.partial(close_kernel, 1.0 / (positions * width * width)),
        out_shape=[shape(grid, f32), shape(term.shape, f32), shape((1, 1), f32)],
        in_specs=vmem_specs(3),
        out_specs=[anywhere] * 3,
        scratch_shapes=[
            pltpu.VMEM(grid, f32), pltpu.VMEM((1, 1), f32), pltpu.SemaphoreType.DMA((3,)),
        ],
    )(grad, probe_gradient, scalars)
    return step.reshape(2, rows, cols), probe_gradient, loss.reshape(())


def local(phase_volume, absorb_volume, probe, amplitudes, scan_rows, scan_cols):
    length = probe.shape[1]
    half = length // 2
    count = scan_rows.shape[2]
    rows, cols = phase_volume.shape[1:]
    sizes = tuple((axis, lax.axis_size(axis)) for axis in ("beam", "row", "col"))
    trans = project(sizes, half, phase_volume, absorb_volume)
    canvas, term, misfit = window_terms(
        trans, probe, amplitudes.reshape(count, length, length),
        scan_rows.reshape(count), scan_cols.reshape(count),
    )
    positions = count * math.prod(size for _, size in sizes)
    return combine(sizes, half, rows, cols, positions, canvas, term, misfit)


def solution(mesh):
    in_specs = (
        P("beam", "row", "col"),
        P("beam", "row", "col"),
        P(),
        P("row", "col", "beam", None, None),
        P("row", "col", "beam"),
        P("row", "col", "beam"),
    )
    out_specs = (P(None, "row", "col"), P(), P())
    return jax.shard_map(local, mesh=mesh, in_specs=in_specs, out_specs=out_specs, check_vma=False)
```

time: 67.9 us -> 59.9 us (0.88)
  Pallas kernels: 59.5 us -> 54.4 us
  between operations: 2.5 us -> 0.74 us
  local copies, waits for them, and re-layouts: 5.62 us -> 4.56 us
    pallas_call x1 -> x2, Pallas kernels: 15.9 us -> 10.5 us  [the longest x1 8.48 us: window_terms(): pl.pallas_call(window_kernel, out_shape=[jax.ShapeDtypeStruct(trans.shape...]
    unnamed x20 -> x22, local copies, waits for them, and re-layouts: 5.11 us -> 4.56 us
where the time goes in v1:
time: 59.9 us; the launch traced here: 59.7 us
  Pallas kernels  54.4 us (91%)
  local copies, waits for them, and re-layouts  4.56 us (8%)
  between operations  0.74 us (1%)
    pallas_call x1, Pallas kernels, combine(): pl.pallas_call(functools.partial(combine_kernel, sizes, half, entries, po...  24.4 us
    pallas_call x1, Pallas kernels, project(): pl.pallas_call(functools.partial(project_kernel, sizes, half), out_shape=...  19.6 us
    pallas_call x1, Pallas kernels, window_terms(): pl.pallas_call(window_kernel, out_shape=[jax.ShapeDtypeStruct(trans.shape...  8.48 us
    unnamed x22, local copies, waits for them, and re-layouts  4.56 us
    pallas_call x1, Pallas kernels, combine(): pl.pallas_call(functools.partial(close_kernel, 1.0 / (positions * width *...  2.01 us

profile of v1, /device:TPU:0, one launch (start us, length us, event | category | flops | bytes accessed | tf_op | source)
XLA Modules:
  0.0 59.7 jit_solution(3778079871358494594)
XLA Ops:
  0.6 0.0 copy-start
  0.6 1.2 %copy-done = bf16[16,256,128]{2,1,0:T(8,128)(2,1)S(1)} copy-done((bf16[16,256,128]{2,1,0:T(8,128)(2,1)S(1)}, bf16[16,256,128]{2,1,0:T(8,128)(2,1)}, u32[]{:S(2)}) %copy-start) | copy-done | bytes 1048600
  1.9 0.0 copy-start.1
  1.9 1.2 %copy-done.1 = bf16[16,256,128]{2,1,0:T(8,128)(2,1)S(1)} copy-done((bf16[16,256,128]{2,1,0:T(8,128)(2,1)S(1)}, bf16[16,256,128]{2,1,0:T(8,128)(2,1)}, u32[]{:S(2)}) %copy-start.1) | copy-done | bytes 1048600
  3.1 0.0 copy-start.2
  3.1 0.0 copy-start.3
  3.1 0.0 copy-start.5
  3.1 0.0 copy-start.9
  3.1 0.0 copy-start.10
  3.1 19.6 %shard_map.103 = f32[2,3,8,64,128]{4,3,2,1,0:T(8,128)S(1)} custom-call(bf16[16,256,128]{2,1,0:T(8,128)(2,1)S(1)} %copy-done, bf16[16,256,128]{2,1,0:T(8,128)(2,1)S(1)} %copy-done.1), custom_call_target="tpu_custom_call" | custom-call | tf_op jit(solution)/shard_map/pallas_call | solution.py:332
  22.7 0.0 copy-done.2
  22.7 0.0 copy-done.3
  22.7 0.0 copy-done.4
  22.7 0.0 copy-done.5
  22.7 0.0 copy-done.9
  22.7 0.0 copy-done.10
  22.7 8.5 %shard_map.104 = (f32[2,3,512,128]{3,2,1,0:T(8,128)S(1)}, f32[2,256,256]{2,1,0:T(8,128)S(1)}, f32[8,256]{1,0:T(8,128)S(1)}) custom-call(s32[8]{0:T(128)S(1)} %bitcast.14, s32[8]{0:T(128)S(1)} %bitcast.15, f32[2,3,512,128]{3,2,1,0:T(8,128)S(1)} %bitcast.9, f32[2,256,256]{2,1,0:T(8,128)S(1)} %copy-done.3, bf16[8,256,256]{2,1,0:T(8,128)(2,1)S(1)} %bitcast.11, ...), custom_call_target="tpu_custom_call" | custom-call | tf_op jit(solution)/shard_map/pallas_call | solution.py:155
  31.2 24.4 %shard_map.105 = (f32[2,2,4,32,128]{4,3,2,1,0:T(8,128)S(1)}, f32[2,4,4,16,256]{4,3,2,1,0:T(8,128)S(1)}, f32[2,8,128]{2,1,0:T(8,128)S(1)}) custom-call(f32[2,3,4,4,32,128]{5,4,3,2,1,0:T(8,128)S(1)} %bitcast.10, f32[2,4,4,16,256]{4,3,2,1,0:T(8,128)S(1)} %bitcast.13, f32[8,256]{1,0:T(8,128)S(1)} %get-tuple-element.14.misfit_ref), custom_call_target="tpu_custom_call" | custom-call | tf_op jit(solution)/shard_map/pallas_call | solution.py:512
  55.6 0.0 copy-start.6
  55.6 0.8 %copy-done.6 = f32[2,4,4,16,256]{4,3,2,1,0:T(8,128)} copy-done((f32[2,4,4,16,256]{4,3,2,1,0:T(8,128)}, f32[2,4,4,16,256]{4,3,2,1,0:T(8,128)S(1)}, u32[]{:S(2)}) %copy-start.6) | copy-done | bytes 524312
  56.4 0.0 copy-start.7
  56.4 0.7 %copy-done.7 = f32[2,2,4,32,128]{4,3,2,1,0:T(8,128)} copy-done((f32[2,2,4,32,128]{4,3,2,1,0:T(8,128)}, f32[2,2,4,32,128]{4,3,2,1,0:T(8,128)S(1)}, u32[]{:S(2)}) %copy-start.7) | copy-done | bytes 262168
  57.1 0.6 %copy-done.8 = f32[2,8,128]{2,1,0:T(8,128)} copy-done((f32[2,8,128]{2,1,0:T(8,128)}, f32[2,8,128]{2,1,0:T(8,128)S(1)}, u32[]{:S(2)}) %copy-start.8) | copy-done | bytes 8216
  57.7 2.0 %shard_map.106 = (f32[2,2,4,32,128]{4,3,2,1,0:T(8,128)}, f32[2,256,256]{2,1,0:T(8,128)}, f32[1,1]{1,0:T(1,128)}) custom-call(f32[2,2,4,32,128]{4,3,2,1,0:T(8,128)} %copy-done.7, f32[2,256,256]{2,1,0:T(8,128)} %bitcast.12, f32[2,8,128]{2,1,0:T(8,128)} %copy-done.8), custom_call_target="tpu_custom_call" | custom-call | tf_op jit(solution)/shard_map/pallas_call | solution.py:537
  (2 shorter events, 0.0 us)
Async XLA Ops:
  0.6 1.2 %copy-start = (bf16[16,256,128]{2,1,0:T(8,128)(2,1)S(1)}, bf16[16,256,128]{2,1,0:T(8,128)(2,1)}, u32[]{:S(2)}) copy-start(bf16[16,256,128]{2,1,0:T(8,128)(2,1)} %phase_ref.1) | copy-start | bytes 3145732
  1.9 1.2 %copy-start.1 = (bf16[16,256,128]{2,1,0:T(8,128)(2,1)S(1)}, bf16[16,256,128]{2,1,0:T(8,128)(2,1)}, u32[]{:S(2)}) copy-start(bf16[16,256,128]{2,1,0:T(8,128)(2,1)} %absorb_ref.1) | copy-start | bytes 3145732
  3.1 19.6 %copy-start.2 = (bf16[1,1,8,256,256]{4,3,2,1,0:T(8,128)(2,1)S(1)}, bf16[1,1,8,256,256]{4,3,2,1,0:T(8,128)(2,1)}, u32[]{:S(2)}) copy-start(bf16[1,1,8,256,256]{4,3,2,1,0:T(8,128)(2,1)} %param.11) | copy-start | bytes 3145732
  3.1 19.6 %copy-start.3 = (f32[2,256,256]{2,1,0:T(8,128)S(1)}, f32[2,256,256]{2,1,0:T(8,128)}, u32[]{:S(2)}) copy-start(f32[2,256,256]{2,1,0:T(8,128)} %probe_ref.1) | copy-start | bytes 1572868
  3.1 19.6 %copy-start.4 = (bf16[512,512]{1,0:T(8,128)(2,1)S(1)}, bf16[512,512]{1,0:T(8,128)(2,1)}, u32[]{:S(2)}) copy-start(bf16[512,512]{1,0:T(8,128)(2,1)} %constant.5.clone.right_ref) | copy-start | bytes 1572868
  3.1 19.6 %copy-start.5 = (bf16[512,512]{1,0:T(8,128)(2,1)S(1)}, bf16[512,512]{1,0:T(8,128)(2,1)}, u32[]{:S(2)}) copy-start(bf16[512,512]{1,0:T(8,128)(2,1)} %constant.4.clone.left_ref) | copy-start | bytes 1572868
  3.1 19.6 %copy-start.9 = (s32[1,1,8]{2,1,0:T(1,128)S(1)}, s32[1,1,8]{2,1,0:T(1,128)}, u32[]{:S(2)}) copy-start(s32[1,1,8]{2,1,0:T(1,128)} %param.12) | copy-start | bytes 100
  3.1 19.6 %copy-start.10 = (s32[1,1,8]{2,1,0:T(1,128)S(1)}, s32[1,1,8]{2,1,0:T(1,128)}, u32[]{:S(2)}) copy-start(s32[1,1,8]{2,1,0:T(1,128)} %param.13) | copy-start | bytes 100
  55.6 0.8 %copy-start.6 = (f32[2,4,4,16,256]{4,3,2,1,0:T(8,128)}, f32[2,4,4,16,256]{4,3,2,1,0:T(8,128)S(1)}, u32[]{:S(2)}) copy-start(f32[2,4,4,16,256]{4,3,2,1,0:T(8,128)S(1)} %get-tuple-element.16) | copy-start | bytes 1572868
  56.4 0.7 %copy-start.7 = (f32[2,2,4,32,128]{4,3,2,1,0:T(8,128)}, f32[2,2,4,32,128]{4,3,2,1,0:T(8,128)S(1)}, u32[]{:S(2)}) copy-start(f32[2,2,4,32,128]{4,3,2,1,0:T(8,128)S(1)} %get-tuple-element.15.grad_ref) | copy-start | bytes 786436
  57.1 0.6 %copy-start.8 = (f32[2,8,128]{2,1,0:T(8,128)}, f32[2,8,128]{2,1,0:T(8,128)S(1)}, u32[]{:S(2)}) copy-start(f32[2,8,128]{2,1,0:T(8,128)S(1)} %get-tuple-element.17.scalar_ref) | copy-start | bytes 24580

commit v2 on v1

v2 whole, which is shorter than its diff:
```python
import functools
import math

import jax
import jax.numpy as jnp
import numpy as np
from jax import lax
from jax.experimental import pallas as pl
from jax.experimental.pallas import tpu as pltpu
from jax.sharding import PartitionSpec as P


def dft_matrices(length):
    indices = np.arange(length, dtype=np.int32)
    product = indices[:, None] * indices[None, :] % length
    angles = product.astype(np.float32) * np.float32(2.0 * math.pi / length)
    factor = np.float32(1.0 / math.sqrt(length))
    real = (np.cos(angles) * factor).astype(jnp.bfloat16)
    imag = (-np.sin(angles) * factor).astype(jnp.bfloat16)
    left = np.block([[real, -imag], [imag, real]])
    right = np.block([[real, imag], [-imag, real]])
    return jnp.asarray(left), jnp.asarray(right)


def partners(me, count):
    if count % 4 == 0:
        high, low = me // 4 * 4 + me % 4 // 2 * 2, me % 2
        flips = [(1, 1), (0, 1), (1, 0)]
        near = []
        for up, across in flips:
            other = me // 4 * 4 + lax.rem(me % 4 // 2 + up, 2) * 2 + lax.rem(low + across, 2)
            near.append(other)
        if count == 4:
            return near
    return [lax.rem(me + d, count) for d in range(1, count)]


class Sends:
    def __init__(self, sizes, send_sem, recv_sem):
        self.axes = {axis: (lax.axis_index(axis), count) for axis, count in sizes}
        self.sends, self.recvs, self.used = send_sem, recv_sem, 0
        self.started = []

    def greet(self, groups):
        barrier = pltpu.get_barrier_semaphore()
        for target in groups:
            pl.semaphore_signal(barrier, inc=1, device_id=target, device_id_type=pl.DeviceIdType.MESH)
        pl.semaphore_wait(barrier, len(groups))

    def others(self, axis):
        return partners(*self.axes[axis])

    def copy(self, target, src, dst):
        index = self.used
        self.used += 1
        return pltpu.make_async_remote_copy(
            src_ref=src, dst_ref=dst, send_sem=self.sends.at[index],
            recv_sem=self.recvs.at[index], device_id=target,
            device_id_type=pl.DeviceIdType.MESH,
        )

    def send(self, target, src, dst):
        one = self.copy(target, src, dst)
        one.start()
        self.started.append(one.wait_send)
        return one

    def sides(self, axis, down, up, to_before=True, to_after=True):
        me, count = self.axes[axis]
        both = jnp.logical_and
        sends_before, sends_after = both(me > 0, to_before), both(me < count - 1, to_after)
        gets_after, gets_before = both(me < count - 1, to_before), both(me > 0, to_after)
        before = self.copy({axis: lax.rem(me + count - 1, count)}, *down)
        after = self.copy({axis: lax.rem(me + 1, count)}, *up)
        pl.when(sends_before)(before.start)
        pl.when(sends_after)(after.start)

        def wait_send():
            pl.when(sends_before)(before.wait_send)
            pl.when(sends_after)(after.wait_send)

        def wait_recv():
            pl.when(gets_after)(before.wait_recv)
            pl.when(gets_before)(after.wait_recv)

        self.started.append(wait_send)
        return wait_recv

    def finish(self):
        for wait_send in self.started:
            wait_send()


def vmem_specs(count):
    return [pl.BlockSpec(memory_space=pltpu.VMEM)] * count


def project(net, half, phase_ref, absorb_ref, out_ref, volume, part, slots, load_sem):
    beam, beams = net.axes["beam"]
    row, rows_count = net.axes["row"]
    depth, rows, cols = phase_ref.shape
    share = rows // beams
    edge = half // share
    blocks = rows // share + 2 * edge
    peers = net.others("beam")
    order = peers + [beam]
    loads = []
    for i, peer in enumerate(order):
        here = pl.ds(pl.multiple_of(peer * share, share), share)
        for plane, ref in enumerate((phase_ref, absorb_ref)):
            one = pltpu.make_async_copy(ref.at[:, here, :], volume.at[plane, i], load_sem.at[plane, i])
            one.start()
            loads.append(one)
    yield
    scatter = []
    for i, peer in enumerate(order):
        for plane in range(2):
            loads[2 * i + plane].wait()
            total = volume[plane, i, 0].astype(jnp.float32)
            for d in range(1, depth):
                total += volume[plane, i, d].astype(jnp.float32)
            part[i, plane] = total
        if i == 0:
            net.greet([{axis: other} for axis in net.axes for other in net.others(axis)])
        if i < beams - 1:
            scatter.append(net.send({"beam": peer}, part.at[i], slots.at[i]))
    total = part[beams - 1]
    for i, one in enumerate(scatter):
        one.wait_recv()
        total += slots[i]
    at = lambda side, block: out_ref.at[:, side, pl.ds(pl.multiple_of(block * share, share), share), :]
    damping = jnp.exp(-total[1])
    own = edge + beam
    here = pl.ds(pl.multiple_of(own * share, share), share)
    out_ref[0, 1, here, :] = damping * jnp.cos(total[0])
    out_ref[1, 1, here, :] = damping * jnp.sin(total[0])
    arrivals = []

    def across(block, when=True):
        arrivals.append(net.sides("col", (at(1, block), at(2, block)), (at(1, block), at(0, block)), when, when))

    def along(share_at):
        here = at(1, edge + share_at)
        below = lax.rem(edge + beams + share_at, blocks)
        above = lax.rem(edge + share_at + blocks - beams, blocks)
        wait = net.sides(
            "row", (here, at(1, below)), (here, at(1, above)), share_at < edge, share_at >= beams - edge
        )
        return wait, share_at, below, above

    gather = [net.send({"beam": peer}, at(1, own), at(1, own)) for peer in peers]
    rims = [along(beam)]
    across(own)
    for peer, one in zip(peers, gather):
        one.wait_recv()
        rims.append(along(peer))
        across(edge + peer)
    for wait, share_at, below, above in rims:
        wait()
        across(below, jnp.logical_and(row < rows_count - 1, share_at < edge))
        across(above, jnp.logical_and(row > 0, share_at >= beams - edge))
    for wait in arrivals:
        wait()
    yield


def windows(
    rows_ref, cols_ref, trans_ref, probe_ref, amplitude_ref, left_ref, right_ref,
    canvas_ref, term_ref, misfit_ref, kept, wave, half, chi, back, moved,
):
    count, length = amplitude_ref.shape[:2]
    lanes = trans_ref.shape[3]
    spans = trans_ref.shape[1]
    inner = length // lanes
    step = 32
    steps = length // step
    dot = functools.partial(jnp.dot, preferred_element_type=jnp.float32)
    lane = lax.broadcasted_iota(jnp.int32, (step, lanes), 1)
    places = moved.shape[0]

    def enter(w, slot, m):
        row_at, col_at = rows_ref[w], cols_ref[w]
        shift = lax.rem(lanes - col_at, lanes)
        keep = lane < lanes - col_at
        here = pl.ds(m * step, step)
        planes = []
        for part in range(2):
            turned = [
                pltpu.roll(trans_ref[part, k, pl.ds(row_at + m * step, step), :], shift, 1)
                for k in range(spans)
            ]
            planes.append([jnp.where(keep, turned[k], turned[k + 1]) for k in range(inner)])
        for k in range(inner):
            real, imag = planes[0][k], planes[1][k]
            at = pl.ds(k * lanes, lanes)
            probe_real, probe_imag = probe_ref[0, here, at], probe_ref[1, here, at]
            kept[slot, 0, here, at] = real
            kept[slot, 1, here, at] = imag
            wave[slot, pl.ds(m * step, step), at] = (probe_real * real - probe_imag * imag).astype(jnp.bfloat16)
            wave[slot, pl.ds(length + m * step, step), at] = (probe_real * imag + probe_imag * real).astype(jnp.bfloat16)

    def compare(w, slot, m, far):
        here = pl.ds(m, step)
        real, imag = far[:, :length], far[:, length:]
        amplitude = amplitude_ref[w, here, :].astype(jnp.float32)
        square = real * real + imag * imag
        inverse = lax.rsqrt(jnp.maximum(square, 1.2e-38))
        off = square * inverse - amplitude
        misfit_ref[...] += jnp.sum((off * off).reshape(step // 8, 8, length), axis=0)
        ratio = 1.0 - amplitude * jnp.minimum(inverse, 2.0)
        chi[slot, here, :] = (real * ratio).astype(jnp.bfloat16)
        chi[slot, pl.ds(length + m, step), :] = (imag * ratio).astype(jnp.bfloat16)

    def leave(w, slot, m, grad):
        col_at = cols_ref[w]
        here = pl.ds(m, step)
        first = lane >= col_at
        objects = [[], []]
        for k in range(inner):
            at = pl.ds(k * lanes, lanes)
            grad_real = grad[:, k * lanes : (k + 1) * lanes]
            grad_imag = grad[:, length + k * lanes : length + (k + 1) * lanes]
            real, imag = kept[slot, 0, here, at], kept[slot, 1, here, at]
            term_real = real * grad_real + imag * grad_imag
            term_imag = real * grad_imag - imag * grad_real
            if w == 0:
                term_ref[0, here, at] = term_real
                term_ref[1, here, at] = term_imag
            else:
                term_ref[0, here, at] += term_real
                term_ref[1, here, at] += term_imag
            probe_real, probe_imag = probe_ref[0, here, at], probe_ref[1, here, at]
            objects[0].append(pltpu.roll(probe_real * term_imag - probe_imag * term_real, col_at, 1))
            objects[1].append(pltpu.roll(probe_real * term_real + probe_imag * term_imag, col_at, 1))
        for part in range(2):
            turned = objects[part]
            for k in range(spans):
                before = turned[k - 1] if k > 0 else 0.0
                after = turned[k] if k < inner else 0.0
                moved[w % places, part, k, pl.ds(length + m, step), :] = jnp.where(first, after, before)

    def left(values, first, out, slot):
        part = dot(first[...], values[slot])
        out[slot, :, :length] = part[:length].astype(jnp.bfloat16)
        out[slot, :, length:] = part[length:].astype(jnp.bfloat16)

    def halves(make, source, table, w, slot, cut):
        tall = length // cut
        for c in range(cut):
            out = dot(source[slot, c * tall : (c + 1) * tall], table[...])
            for m in range(tall // step):
                make(w, slot, c * tall + m * step, out[m * step : (m + 1) * step])

    def enters(w):
        if w < count:
            for m in range(steps):
                enter(w, w % 2, m)

    def place(pair, block, b, k):
        thin = canvas_ref.shape[4]
        start = length + (block * canvas_ref.shape[3] + b) * thin
        for part in range(2):
            total = None if pair == 0 else canvas_ref[part, k, block, b]
            for w in (2 * pair, 2 * pair + 1):
                piece = moved[w % places, part, k, pl.ds(start - rows_ref[w], thin), :]
                total = piece if total is None else total + piece
            canvas_ref[part, k, block, b] = total

    pairs = count // 2
    enters(0)
    for p in range(pairs):
        a, b = 2 * p, 2 * p + 1
        left(wave, left_ref, half, 0)
        if p:
            halves(leave, back, left_ref, b - 2, 1, 2)
        enters(b)
        left(wave, left_ref, half, 1)
        halves(compare, half, right_ref, a, 0, 2)
        left(chi, right_ref, back, 0)
        if p:
            for block in range(canvas_ref.shape[2]):
                for share in range(canvas_ref.shape[3]):
                    for k in range(spans):
                        place(p - 1, block, share, k)
        halves(compare, half, right_ref, b, 1, 2)
        left(chi, right_ref, back, 1)
        halves(leave, back, left_ref, a, 0, 2)
        enters(a + 2)
    halves(leave, back, left_ref, count - 1, 1, 2)
    return functools.partial(place, pairs - 1)


def combine(
    net, place, entries, positions, canvas_ref, term_ref, misfit_ref,
    step_ref, probe_ref, loss_ref,
    pieces, side, strip, rims, folded, folded_in, grads,
    term_col, term_a, term_in, small, small_col,
):
    beam, beams = net.axes["beam"]
    row, rows_count = net.axes["row"]
    col, cols_count = net.axes["col"]
    blocks = strip.shape[1]
    cols = strip.shape[4]
    beam_peers, col_peers = net.others("beam"), net.others("col")
    order = beam_peers + [beam]
    wide = [(b, r) for b in order for r in net.others("row") + [row]][:-1]
    to = lambda b, r: {"beam": b, "row": r}

    lines = pieces.shape[3]
    for c in range(cols_count):
        for b in range(beams):
            for r in range(rows_count):
                at = ((c * beams + b) * rows_count + r) * lines
                pieces[c, b, r] = term_ref[at // term_ref.shape[1], pl.ds(at % term_ref.shape[1], lines), :]
    term_copies = [net.send({"col": c}, pieces.at[c], term_col.at[k]) for k, c in enumerate(col_peers)]
    across = []
    for p in order:
        for block in range(blocks):
            place(block, p, 0)
            place(block, p, 2)
        across.append(net.sides(
            "col",
            (canvas_ref.at[:, 0, :, p], side.at[1, :, :, p]),
            (canvas_ref.at[:, 2, :, p], side.at[0, :, :, p]),
        ))
    for p in order:
        for block in range(blocks):
            place(block, p, 1)
    for one in term_copies:
        one.wait_recv()
    total = pieces[col]
    for k in range(cols_count - 1):
        total += term_col[k]
    term_a[...] = total
    term_copies = [net.send(to(b, r), term_a.at[b, r], term_in.at[i]) for i, (b, r) in enumerate(wide)]

    along = []
    for i, p in enumerate(order):
        across[i]()
        strip[:, :, p] = canvas_ref[:, 1, :, p] + side[0, :, :, p] + side[1, :, :, p]
        along.append(net.sides(
            "row",
            (strip.at[:, 0, p], rims.at[1, :, p]),
            (strip.at[:, blocks - 1, p], rims.at[0, :, p]),
        ))
    grids = []
    for i, p in enumerate(order):
        along[i]()
        folded[i] = strip[:, 1 : blocks - 1, p]
        folded[i, :, 0] += rims[0, :, p]
        folded[i, :, blocks - 3] += rims[1, :, p]
        if i < beams - 1:
            grids.append(net.send({"beam": p}, folded.at[i], folded_in.at[i]))

    total = term_a[beam, row]
    for i, one in enumerate(term_copies):
        one.wait_recv()
        total += term_in[i]
    probe_ref[col, beam, row] = total * (1.0 / positions)
    mine = probe_ref.at[col, beam, row]
    term_copies = [net.send(to(b, r), mine, mine) for b, r in wide]
    total = folded[beams - 1]
    for i, one in enumerate(grids):
        one.wait_recv()
        total += folded_in[i]
    grads[0, :, beam] = total[0]
    grads[1, :, beam] = -total[1]
    misfit_sum = misfit_ref[:, :cols]
    for k in range(1, misfit_ref.shape[1] // cols):
        misfit_sum += misfit_ref[:, k * cols : (k + 1) * cols]
    small[beam, row, 0] = jnp.sum((total * total).reshape(-1, 8, cols), axis=0)
    small[beam, row, 1] = misfit_sum
    mine = small.at[beam, row]
    smalls = [net.send(to(b, r), mine, mine) for b, r in wide]
    mine = grads.at[:, :, beam]
    grid_copies = [net.send({"beam": p}, mine, mine) for p in beam_peers]
    col_copies = []
    for i, p in enumerate(order):
        for one in term_copies[i * rows_count : (i + 1) * rows_count]:
            one.wait_recv()
        mine = probe_ref.at[col, p]
        col_copies += [net.send({"col": c}, mine, mine) for c in col_peers]
    for one in smalls:
        one.wait_recv()
    total = small[0, 0]
    for k in range(1, beams * rows_count):
        total += small[k // rows_count, k % rows_count]
    small_col[col] = total
    smalls = [net.send({"col": c}, small_col.at[col], small_col.at[col]) for c in col_peers]
    for one in grid_copies + smalls:
        one.wait_recv()
    total = small_col[0]
    for k in range(1, cols_count):
        total += small_col[k]
    mean_square = jnp.sum(total[0], keepdims=True) / entries
    factor = jnp.minimum(1.0, 0.5 / jnp.sqrt(mean_square + 1e-06))
    step_ref[...] = grads[...] * factor[None, None, None]
    loss_ref[...] = jnp.sum(total[1], keepdims=True) * (1.0 / (positions * misfit_ref.shape[1] ** 2))
    for one in col_copies:
        one.wait_recv()
    net.finish()


def whole_kernel(
    sizes, half_length, entries, positions,
    rows_in, cols_in, phase_ref, absorb_ref, probe_in, amplitude_in, left_in, right_in,
    step_ref, probe_out, loss_ref,
    rows_ref, cols_ref, volume, part, slots, trans, probe, amplitude, left, right,
    kept, wave, half, chi, back, moved, canvas, term, misfit,
    pieces, side, strip, rims, folded, folded_in, grads,
    term_col, term_a, term_in, small, small_col,
    load_sem, early_sem, send_sem, recv_sem,
):
    net = Sends(sizes, send_sem, recv_sem)
    col, cols_count = net.axes["col"]
    stages = project(net, half_length, phase_ref, absorb_ref, trans, volume, part, slots, load_sem)
    next(stages)
    early = [
        pltpu.make_async_copy(src, dst, early_sem.at[k])
        for k, (src, dst) in enumerate(
            (
                (rows_in, rows_ref), (cols_in, cols_ref), (probe_in, probe),
                (left_in, left), (amplitude_in, amplitude), (right_in, right),
            )
        )
    ]
    for one in early:
        one.start()
    trans[0] = jnp.ones(trans.shape[1:], jnp.float32)
    trans[1] = jnp.zeros(trans.shape[1:], jnp.float32)
    rims[...] = jnp.zeros_like(rims)
    misfit[...] = jnp.zeros_like(misfit)

    @pl.when(col == 0)
    def _():
        side[0] = jnp.zeros(side.shape[1:], jnp.float32)

    @pl.when(col == cols_count - 1)
    def _():
        side[1] = jnp.zeros(side.shape[1:], jnp.float32)

    length = probe.shape[1]
    blank = jnp.zeros(moved.shape[1:3] + (length, moved.shape[4]), jnp.float32)
    for k in range(moved.shape[0]):
        moved[k, :, :, :length, :] = blank
        moved[k, :, :, 2 * length :, :] = blank
    next(stages)
    for one in early:
        one.wait()
    place = windows(
        rows_ref, cols_ref, trans, probe, amplitude, left, right,
        canvas, term, misfit, kept, wave, half, chi, back, moved,
    )
    combine(
        net, place, entries, positions, canvas, term, misfit, step_ref, probe_out, loss_ref,
        pieces, side, strip, rims, folded, folded_in, grads,
        term_col, term_a, term_in, small, small_col,
    )


def pin(x):
    return pltpu.with_memory_space_constraint(x, pltpu.HBM)


def local(phase_volume, absorb_volume, probe, amplitudes, scan_rows, scan_cols):
    length = probe.shape[1]
    half = length // 2
    count = scan_rows.shape[2]
    depth, rows, cols = phase_volume.shape
    sizes = tuple((axis, lax.axis_size(axis)) for axis in ("beam", "row", "col"))
    counts = dict(sizes)
    beams, rows_count, cols_count = counts["beam"], counts["row"], counts["col"]
    positions = count * beams * rows_count * cols_count
    assert half == cols and count % 2 == 0
    left, right = dft_matrices(length)
    f32, bf16 = jnp.float32, jnp.bfloat16
    share = rows // beams
    tall = rows + 2 * half
    blocks = tall // half
    thin = half // beams
    lines = 2 * length // (cols_count * beams * rows_count)
    shape = (cols_count, beams, rows_count, lines, length)
    grid = (2, blocks - 2, beams, thin, cols)
    entries = 2 * rows * cols * rows_count * cols_count
    wide = beams * rows_count
    wires = 10 * beams + (cols_count + 1) + 2 * beams + wide + 2 * beams + 2 * wide + beams * (cols_count + 1) + cols_count + 16
    vmem = pltpu.VMEM
    hbm = pl.BlockSpec(memory_space=pltpu.HBM)
    step, probe_gradient, loss = pl.pallas_call(
        functools.partial(whole_kernel, sizes, half, entries, positions),
        out_shape=[jax.ShapeDtypeStruct(s, f32) for s in (grid, shape, (1, 1))],
        in_specs=[hbm] * 8,
        out_specs=vmem_specs(3),
        scratch_shapes=[
            pltpu.SMEM((count,), jnp.int32),
            pltpu.SMEM((count,), jnp.int32),
            vmem((2, beams, depth, share, cols), phase_volume.dtype),
            vmem((beams, 2, share, cols), f32),
            vmem((beams - 1, 2, share, cols), f32),
            vmem((2, 3, tall, cols), f32),
            vmem(probe.shape, f32),
            vmem((count, length, length), amplitudes.dtype),
            vmem(left.shape, bf16),
            vmem(right.shape, bf16),
            vmem((2, 2, length, length), f32),
            vmem((2, 2 * length, length), bf16),
            vmem((2, length, 2 * length), bf16),
            vmem((2, 2 * length, length), bf16),
            vmem((2, length, 2 * length), bf16),
            vmem((4, 2, 3, 3 * length, cols), f32),
            vmem((2, 3, blocks, beams, thin, cols), f32),
            vmem(probe.shape, f32),
            vmem((8, length), f32),
            vmem(shape, f32),
            vmem((2, 2, blocks, beams, thin, cols), f32),
            vmem((2, blocks, beams, thin, cols), f32),
            vmem((2, 2, beams, thin, cols), f32),
            vmem((beams, 2, blocks - 2, thin, cols), f32),
            vmem((beams - 1, 2, blocks - 2, thin, cols), f32),
            vmem(grid, f32),
            vmem((cols_count - 1,) + shape[1:], f32),
            vmem(shape[1:], f32),
            vmem((wide - 1,) + shape[3:], f32),
            vmem((beams, rows_count, 2, 8, cols), f32),
            vmem((cols_count, 2, 8, cols), f32),
            pltpu.SemaphoreType.DMA((2, beams)),
            pltpu.SemaphoreType.DMA((6,)),
            pltpu.SemaphoreType.DMA((wires,)),
            pltpu.SemaphoreType.DMA((wires,)),
        ],
        compiler_params=pltpu.CompilerParams(
            collective_id=1, has_side_effects=True, vmem_limit_bytes=48 * 2**20
        ),
    )(
        pin(scan_rows.reshape(count)), pin(scan_cols.reshape(count)), pin(phase_volume), pin(absorb_volume), pin(probe),
        pin(amplitudes.reshape(count, length, length)), pin(left), pin(right),
    )
    return step.reshape(2, rows, cols), probe_gradient.reshape(probe.shape), loss.reshape(())


def solution(mesh):
    in_specs = (
        P("beam", "row", "col"),
        P("beam", "row", "col"),
        P(),
        P("row", "col", "beam", None, None),
        P("row", "col", "beam"),
        P("row", "col", "beam"),
    )
    out_specs = (P(None, "row", "col"), P(), P())
    return jax.shard_map(local, mesh=mesh, in_specs=in_specs, out_specs=out_specs, check_vma=False)
```

time: 59.9 us -> 57.5 us (0.960)
  local copies, waits for them, and re-layouts: 4.56 us -> 1.5 us
  between operations: 0.74 us -> 2.33 us
  Pallas kernels: 54.4 us -> 53.4 us
    unnamed x22 -> x2, local copies, waits for them, and re-layouts: 4.56 us -> 1.5 us
    pallas_call x4 -> x1, Pallas kernels: 54.4 us -> 53.4 us  [local(): pl.pallas_call(functools.partial(whole_kernel, sizes, half, entries, posi...]
where the time goes in v2:
time: 57.5 us; the launch traced here: 57.2 us
  Pallas kernels  53.4 us (93%)
  between operations  2.33 us (4%)
  local copies, waits for them, and re-layouts  1.5 us (3%)
    pallas_call x1, Pallas kernels, local(): pl.pallas_call(functools.partial(whole_kernel, sizes, half, entries, posi...  53.4 us
    unnamed x2, local copies, waits for them, and re-layouts  1.5 us

profile of v2, /device:TPU:0, one launch (start us, length us, event | category | flops | bytes accessed | tf_op | source)
XLA Modules:
  0.0 57.2 jit_solution(13897926455965309174)
XLA Ops:
  0.6 53.4 %shard_map.103 = (f32[2,2,4,32,128]{4,3,2,1,0:T(8,128)S(1)}, f32[2,4,4,16,256]{4,3,2,1,0:T(8,128)S(1)}, f32[1,1]{1,0:T(1,128)}) custom-call(s32[8]{0:T(128)} %bitcast.9, s32[8]{0:T(128)} %bitcast.10, bf16[16,256,128]{2,1,0:T(8,128)(2,1)} %phase_ref.1, bf16[16,256,128]{2,1,0:T(8,128)(2,1)} %absorb_ref.1, f32[2,256,256]{2,1,0:T(8,128)} %probe_in.1, ...), custom_call_target="tpu_custom_call" | custom-call | tf_op jit(solution)/shard_map/pallas_call | solution.py:489
  54.0 0.7 %copy.14 = f32[2,256,128]{2,1,0:T(8,128)} copy(f32[2,256,128]{2,1,0:T(8,128)S(1)} %bitcast.7) | data formatting | bytes 524288
  54.7 0.8 %copy.15 = f32[2,256,256]{2,1,0:T(8,128)} copy(f32[2,256,256]{2,1,0:T(8,128)S(1)} %bitcast.6) | data formatting | bytes 1048576

commit v3 on v2

--- a/solution.py
+++ b/solution.py
@@ -38,23 +38,28 @@
 class Sends:
     def __init__(self, sizes, send_sem, recv_sem):
         self.axes = {axis: (lax.axis_index(axis), count) for axis, count in sizes}
-        self.sends, self.recvs, self.used = send_sem, recv_sem, 0
+        self.sends, self.recvs = send_sem, recv_sem
+        self.used = self.base = 0
         self.started = []
 
-    def greet(self, groups):
-        barrier = pltpu.get_barrier_semaphore()
-        for target in groups:
-            pl.semaphore_signal(barrier, inc=1, device_id=target, device_id_type=pl.DeviceIdType.MESH)
-        pl.semaphore_wait(barrier, len(groups))
+    def greet(self):
+        self.barrier = pltpu.get_barrier_semaphore()
+        targets = [{axis: other} for axis in self.axes for other in self.others(axis)]
+        for target in targets:
+            pl.semaphore_signal(self.barrier, inc=1, device_id=target, device_id_type=pl.DeviceIdType.MESH)
+        return lambda: pl.semaphore_wait(self.barrier, len(targets))
 
     def others(self, axis):
         return partners(*self.axes[axis])
 
-    def copy(self, target, src, dst):
-        index = self.used
+    def take(self):
         self.used += 1
+        return self.used - 1
+
+    def copy(self, target, src, dst, index=None):
+        index = self.take() if index is None else index
         return pltpu.make_async_remote_copy(
-            src_ref=src, dst_ref=dst, send_sem=self.sends.at[index],
+            src_ref=src, dst_ref=dst, send_sem=self.sends.at[index - self.base],
             recv_sem=self.recvs.at[index], device_id=target,
             device_id_type=pl.DeviceIdType.MESH,
         )
@@ -65,13 +70,21 @@
         self.started.append(one.wait_send)
         return one
 
-    def sides(self, axis, down, up, to_before=True, to_after=True):
+    def group(self, targets, src, slots):
+        index = self.take()
+        for k, target in enumerate(targets):
+            self.copy(target, src, slots.at[k], index).start()
+        self.started.append(pltpu.make_async_copy(slots, slots, self.sends.at[index - self.base]).wait)
+        return pltpu.make_async_copy(slots, slots, self.recvs.at[index]).wait
+
+    def sides(self, axis, down, up, to_before=True, to_after=True, one_way=False, index=None):
         me, count = self.axes[axis]
         both = jnp.logical_and
         sends_before, sends_after = both(me > 0, to_before), both(me < count - 1, to_after)
         gets_after, gets_before = both(me < count - 1, to_before), both(me > 0, to_after)
-        before = self.copy({axis: lax.rem(me + count - 1, count)}, *down)
-        after = self.copy({axis: lax.rem(me + 1, count)}, *up)
+        index = self.take() if index is None else index
+        before = self.copy({axis: lax.rem(me + count - 1, count)}, *down, index)
+        after = self.copy({axis: lax.rem(me + 1, count)}, *up, index if one_way or count == 2 else self.take())
         pl.when(sends_before)(before.start)
         pl.when(sends_after)(after.start)
 
@@ -89,6 +102,14 @@
     def finish(self):
         for wait_send in self.started:
             wait_send()
+        self.started = []
+        self.base = self.used
+
+
+def tree(values):
+    if len(values) == 4:
+        return (values[3] + values[1]) + (values[2] + values[0])
+    return functools.reduce(lambda a, b: a + b, values)
 
 
 def vmem_specs(count):
@@ -102,26 +123,25 @@
     share = rows // beams
     edge = half // share
     blocks = rows // share + 2 * edge
+    one_way = 2 * edge <= beams
     peers = net.others("beam")
     order = peers + [beam]
-    loads = []
     for i, peer in enumerate(order):
         here = pl.ds(pl.multiple_of(peer * share, share), share)
         for plane, ref in enumerate((phase_ref, absorb_ref)):
-            one = pltpu.make_async_copy(ref.at[:, here, :], volume.at[plane, i], load_sem.at[plane, i])
-            one.start()
-            loads.append(one)
+            pltpu.make_async_copy(ref.at[:, here, :], volume.at[i, plane], load_sem.at[i]).start()
+    arrived = net.greet()
     yield
     scatter = []
     for i, peer in enumerate(order):
+        pltpu.make_async_copy(volume.at[i], volume.at[i], load_sem.at[i]).wait()
         for plane in range(2):
-            loads[2 * i + plane].wait()
-            total = volume[plane, i, 0].astype(jnp.float32)
+            total = volume[i, plane, 0].astype(jnp.float32)
             for d in range(1, depth):
-                total += volume[plane, i, d].astype(jnp.float32)
+                total += volume[i, plane, d].astype(jnp.float32)
             part[i, plane] = total
         if i == 0:
-            net.greet([{axis: other} for axis in net.axes for other in net.others(axis)])
+            arrived()
         if i < beams - 1:
             scatter.append(net.send({"beam": peer}, part.at[i], slots.at[i]))
     total = part[beams - 1]
@@ -136,15 +156,18 @@
     out_ref[1, 1, here, :] = damping * jnp.sin(total[0])
     arrivals = []
 
-    def across(block, when=True):
-        arrivals.append(net.sides("col", (at(1, block), at(2, block)), (at(1, block), at(0, block)), when, when))
+    def across(block, when=True, index=None):
+        arrivals.append(net.sides(
+            "col", (at(1, block), at(2, block)), (at(1, block), at(0, block)), when, when, index=index
+        ))
 
     def along(share_at):
         here = at(1, edge + share_at)
         below = lax.rem(edge + beams + share_at, blocks)
         above = lax.rem(edge + share_at + blocks - beams, blocks)
         wait = net.sides(
-            "row", (here, at(1, below)), (here, at(1, above)), share_at < edge, share_at >= beams - edge
+            "row", (here, at(1, below)), (here, at(1, above)), share_at < edge, share_at >= beams - edge,
+            one_way=one_way,
         )
         return wait, share_at, below, above
 
@@ -157,10 +180,12 @@
         across(edge + peer)
     for wait, share_at, below, above in rims:
         wait()
+        index = net.used if one_way and net.axes["col"][1] == 2 else None
         across(below, jnp.logical_and(row < rows_count - 1, share_at < edge))
-        across(above, jnp.logical_and(row > 0, share_at >= beams - edge))
+        across(above, jnp.logical_and(row > 0, share_at >= beams - edge), index)
     for wait in arrivals:
         wait()
+    net.finish()
     yield
 
 
@@ -213,7 +238,7 @@
 
     def leave(w, slot, m, grad):
         col_at = cols_ref[w]
-        here = pl.ds(m, step)
+        here, low = pl.ds(m, step), pl.ds(length + m, step)
         first = lane >= col_at
         objects = [[], []]
         for k in range(inner):
@@ -224,11 +249,11 @@
             term_real = real * grad_real + imag * grad_imag
             term_imag = real * grad_imag - imag * grad_real
             if w == 0:
-                term_ref[0, here, at] = term_real
-                term_ref[1, here, at] = term_imag
+                term_ref[here, at] = term_real
+                term_ref[low, at] = term_imag
             else:
-                term_ref[0, here, at] += term_real
-                term_ref[1, here, at] += term_imag
+                term_ref[here, at] += term_real
+                term_ref[low, at] += term_imag
             probe_real, probe_imag = probe_ref[0, here, at], probe_ref[1, here, at]
             objects[0].append(pltpu.roll(probe_real * term_imag - probe_imag * term_real, col_at, 1))
             objects[1].append(pltpu.roll(probe_real * term_real + probe_imag * term_imag, col_at, 1))
@@ -293,26 +318,24 @@
 def combine(
     net, place, entries, positions, canvas_ref, term_ref, misfit_ref,
     step_ref, probe_ref, loss_ref,
-    pieces, side, strip, rims, folded, folded_in, grads,
-    term_col, term_a, term_in, small, small_col,
+    side, strip, rims, folded, folded_in, grads,
+    term_col, term_a, term_beam, term_b, term_row, small, small_in, small_all,
 ):
     beam, beams = net.axes["beam"]
     row, rows_count = net.axes["row"]
     col, cols_count = net.axes["col"]
     blocks = strip.shape[1]
     cols = strip.shape[4]
-    beam_peers, col_peers = net.others("beam"), net.others("col")
+    lines = term_b.shape[0]
+    beam_peers, row_peers, col_peers = (net.others(axis) for axis in ("beam", "row", "col"))
     order = beam_peers + [beam]
-    wide = [(b, r) for b in order for r in net.others("row") + [row]][:-1]
-    to = lambda b, r: {"beam": b, "row": r}
-
-    lines = pieces.shape[3]
-    for c in range(cols_count):
-        for b in range(beams):
-            for r in range(rows_count):
-                at = ((c * beams + b) * rows_count + r) * lines
-                pieces[c, b, r] = term_ref[at // term_ref.shape[1], pl.ds(at % term_ref.shape[1], lines), :]
-    term_copies = [net.send({"col": c}, pieces.at[c], term_col.at[k]) for k, c in enumerate(col_peers)]
+    wide = [{"beam": b, "row": r} for b in order for r in row_peers + [row]][:-1]
+    rows_of = lambda c, b, n: pl.ds(pl.multiple_of((c * beams + b) * lines, lines), n * lines)
+
+    term_copies = [
+        net.send({"col": c}, term_ref.at[rows_of(c, 0, beams), :], term_col.at[k])
+        for k, c in enumerate(col_peers)
+    ]
     across = []
     for p in order:
         for block in range(blocks):
@@ -328,11 +351,14 @@
             place(block, p, 1)
     for one in term_copies:
         one.wait_recv()
-    total = pieces[col]
-    for k in range(cols_count - 1):
-        total += term_col[k]
-    term_a[...] = total
-    term_copies = [net.send(to(b, r), term_a.at[b, r], term_in.at[i]) for i, (b, r) in enumerate(wide)]
+    term_beams = []
+    for i, p in enumerate(order):
+        total = term_ref[rows_of(col, p, 1), :]
+        for k in range(cols_count - 1):
+            total += term_col[k, pl.ds(pl.multiple_of(p * lines, lines), lines), :]
+        term_a[i] = total
+        if i < beams - 1:
+            term_beams.append(net.send({"beam": p}, term_a.at[i], term_beam.at[i]))
 
     along = []
     for i, p in enumerate(order):
@@ -352,13 +378,13 @@
         if i < beams - 1:
             grids.append(net.send({"beam": p}, folded.at[i], folded_in.at[i]))
 
-    total = term_a[beam, row]
-    for i, one in enumerate(term_copies):
-        one.wait_recv()
-        total += term_in[i]
-    probe_ref[col, beam, row] = total * (1.0 / positions)
-    mine = probe_ref.at[col, beam, row]
-    term_copies = [net.send(to(b, r), mine, mine) for b, r in wide]
+    total = term_a[beams - 1]
+    for i, one in enumerate(term_beams):
+        one.wait_recv()
+        total += term_beam[i]
+    term_b[...] = total
+    term_rows = [net.send({"row": r}, term_b, term_row.at[k]) for k, r in enumerate(row_peers)]
+
     total = folded[beams - 1]
     for i, one in enumerate(grids):
         one.wait_recv()
@@ -368,30 +394,31 @@
     misfit_sum = misfit_ref[:, :cols]
     for k in range(1, misfit_ref.shape[1] // cols):
         misfit_sum += misfit_ref[:, k * cols : (k + 1) * cols]
-    small[beam, row, 0] = jnp.sum((total * total).reshape(-1, 8, cols), axis=0)
-    small[beam, row, 1] = misfit_sum
-    mine = small.at[beam, row]
-    smalls = [net.send(to(b, r), mine, mine) for b, r in wide]
+    small[0] = jnp.sum((total * total).reshape(-1, 8, cols), axis=0)
+    small[1] = misfit_sum
+    small_wait = net.group(wide, small, small_in)
     mine = grads.at[:, :, beam]
     grid_copies = [net.send({"beam": p}, mine, mine) for p in beam_peers]
-    col_copies = []
-    for i, p in enumerate(order):
-        for one in term_copies[i * rows_count : (i + 1) * rows_count]:
-            one.wait_recv()
-        mine = probe_ref.at[col, p]
-        col_copies += [net.send({"col": c}, mine, mine) for c in col_peers]
-    for one in smalls:
-        one.wait_recv()
-    total = small[0, 0]
-    for k in range(1, beams * rows_count):
-        total += small[k // rows_count, k % rows_count]
-    small_col[col] = total
-    smalls = [net.send({"col": c}, small_col.at[col], small_col.at[col]) for c in col_peers]
+
+    for one in term_rows:
+        one.wait_recv()
+    total = tree([term_row[k] for k in range(rows_count - 1)] + [term_b[...]])
+    probe_ref[rows_of(col, beam, 1), :] = total * (1.0 / positions)
+    share = lambda p: probe_ref.at[rows_of(col, p, 1), :]
+    term_copies = [net.send({"beam": p}, share(beam), share(beam)) for p in beam_peers]
+    col_copies = [net.send({"col": c}, share(beam), share(beam)) for c in col_peers]
+    small_wait()
+    sums = [small_in[k] for k in range(beams * rows_count - 1)] + [small[...]]
+    small_all[col] = tree([tree(sums[b * rows_count : (b + 1) * rows_count]) for b in range(beams)])
+    smalls = [net.send({"col": c}, small_all.at[col], small_all.at[col]) for c in col_peers]
+    for p, one in zip(beam_peers, term_copies):
+        one.wait_recv()
+        col_copies += [net.send({"col": c}, share(p), share(p)) for c in col_peers]
     for one in grid_copies + smalls:
         one.wait_recv()
-    total = small_col[0]
+    total = small_all[0]
     for k in range(1, cols_count):
-        total += small_col[k]
+        total += small_all[k]
     mean_square = jnp.sum(total[0], keepdims=True) / entries
     factor = jnp.minimum(1.0, 0.5 / jnp.sqrt(mean_square + 1e-06))
     step_ref[...] = grads[...] * factor[None, None, None]
@@ -399,6 +426,7 @@
     for one in col_copies:
         one.wait_recv()
     net.finish()
+    assert net.used == net.recvs.shape[0]
 
 
 def whole_kernel(
@@ -407,11 +435,12 @@
     step_ref, probe_out, loss_ref,
     rows_ref, cols_ref, volume, part, slots, trans, probe, amplitude, left, right,
     kept, wave, half, chi, back, moved, canvas, term, misfit,
-    pieces, side, strip, rims, folded, folded_in, grads,
-    term_col, term_a, term_in, small, small_col,
+    side, strip, rims, folded, folded_in, grads,
+    term_col, term_a, term_beam, term_b, term_row, small, small_in, small_all,
     load_sem, early_sem, send_sem, recv_sem,
 ):
     net = Sends(sizes, send_sem, recv_sem)
+    row, rows_count = net.axes["row"]
     col, cols_count = net.axes["col"]
     stages = project(net, half_length, phase_ref, absorb_ref, trans, volume, part, slots, load_sem)
     next(stages)
@@ -426,18 +455,27 @@
     ]
     for one in early:
         one.start()
-    trans[0] = jnp.ones(trans.shape[1:], jnp.float32)
-    trans[1] = jnp.zeros(trans.shape[1:], jnp.float32)
-    rims[...] = jnp.zeros_like(rims)
     misfit[...] = jnp.zeros_like(misfit)
 
-    @pl.when(col == 0)
-    def _():
-        side[0] = jnp.zeros(side.shape[1:], jnp.float32)
-
-    @pl.when(col == cols_count - 1)
-    def _():
-        side[1] = jnp.zeros(side.shape[1:], jnp.float32)
+    def empty(where):
+        trans[(0,) + where] = jnp.ones_like(trans[(0,) + where])
+        trans[(1,) + where] = jnp.zeros_like(trans[(1,) + where])
+
+    for k, at in ((0, 0), (1, cols_count - 1)):
+
+        @pl.when(col == at)
+        def _():
+            side[k] = jnp.zeros(side.shape[1:], jnp.float32)
+            empty((2 * k,))
+
+    for k, at in ((0, 0), (1, rows_count - 1)):
+
+        @pl.when(row == at)
+        def _():
+            rims[k] = jnp.zeros(rims.shape[1:], jnp.float32)
+            begin = k * (trans.shape[2] - half_length)
+            for j in range(3):
+                empty((j, pl.ds(begin, half_length)))
 
     length = probe.shape[1]
     blank = jnp.zeros(moved.shape[1:3] + (length, moved.shape[4]), jnp.float32)
@@ -453,8 +491,8 @@
     )
     combine(
         net, place, entries, positions, canvas, term, misfit, step_ref, probe_out, loss_ref,
-        pieces, side, strip, rims, folded, folded_in, grads,
-        term_col, term_a, term_in, small, small_col,
+        side, strip, rims, folded, folded_in, grads,
+        term_col, term_a, term_beam, term_b, term_row, small, small_in, small_all,
     )
 
 
@@ -478,23 +516,26 @@
     tall = rows + 2 * half
     blocks = tall // half
     thin = half // beams
-    lines = 2 * length // (cols_count * beams * rows_count)
-    shape = (cols_count, beams, rows_count, lines, length)
+    chunk = 2 * length // cols_count
+    lines = chunk // beams
     grid = (2, blocks - 2, beams, thin, cols)
     entries = 2 * rows * cols * rows_count * cols_count
-    wide = beams * rows_count
-    wires = 10 * beams + (cols_count + 1) + 2 * beams + wide + 2 * beams + 2 * wide + beams * (cols_count + 1) + cols_count + 16
+    ways = 1 if cols_count == 2 else 2
+    one_way = 2 * half <= rows
+    early = 2 * (beams - 1) + (1 if one_way else 2) * beams
+    early += beams * (2 if one_way and ways == 1 else 3 * ways)
+    late = (cols_count - 1) * (2 + beams) + (ways + 2) * beams + 4 * (beams - 1) + rows_count
     vmem = pltpu.VMEM
     hbm = pl.BlockSpec(memory_space=pltpu.HBM)
     step, probe_gradient, loss = pl.pallas_call(
         functools.partial(whole_kernel, sizes, half, entries, positions),
-        out_shape=[jax.ShapeDtypeStruct(s, f32) for s in (grid, shape, (1, 1))],
+        out_shape=[jax.ShapeDtypeStruct(s, f32) for s in (grid, (2 * length, length), (1, 1))],
         in_specs=[hbm] * 8,
         out_specs=vmem_specs(3),
         scratch_shapes=[
             pltpu.SMEM((count,), jnp.int32),
             pltpu.SMEM((count,), jnp.int32),
-            vmem((2, beams, depth, share, cols), phase_volume.dtype),
+            vmem((beams, 2, depth, share, cols), phase_volume.dtype),
             vmem((beams, 2, share, cols), f32),
             vmem((beams - 1, 2, share, cols), f32),
             vmem((2, 3, tall, cols), f32),
@@ -509,24 +550,26 @@
             vmem((2, length, 2 * length), bf16),
             vmem((4, 2, 3, 3 * length, cols), f32),
             vmem((2, 3, blocks, beams, thin, cols), f32),
-            vmem(probe.shape, f32),
+            vmem((2 * length, length), f32),
             vmem((8, length), f32),
-            vmem(shape, f32),
             vmem((2, 2, blocks, beams, thin, cols), f32),
             vmem((2, blocks, beams, thin, cols), f32),
             vmem((2, 2, beams, thin, cols), f32),
             vmem((beams, 2, blocks - 2, thin, cols), f32),
             vmem((beams - 1, 2, blocks - 2, thin, cols), f32),
             vmem(grid, f32),
-            vmem((cols_count - 1,) + shape[1:], f32),
-            vmem(shape[1:], f32),
-            vmem((wide - 1,) + shape[3:], f32),
-            vmem((beams, rows_count, 2, 8, cols), f32),
+            vmem((cols_count - 1, chunk, length), f32),
+            vmem((beams, lines, length), f32),
+            vmem((beams - 1, lines, length), f32),
+            vmem((lines, length), f32),
+            vmem((rows_count - 1, lines, length), f32),
+            vmem((2, 8, cols), f32),
+            vmem((beams * rows_count - 1, 2, 8, cols), f32),
             vmem((cols_count, 2, 8, cols), f32),
-            pltpu.SemaphoreType.DMA((2, beams)),
+            pltpu.SemaphoreType.DMA((beams,)),
             pltpu.SemaphoreType.DMA((6,)),
-            pltpu.SemaphoreType.DMA((wires,)),
-            pltpu.SemaphoreType.DMA((wires,)),
+            pltpu.SemaphoreType.DMA((max(early, late),)),
+            pltpu.SemaphoreType.DMA((early + late,)),
         ],
         compiler_params=pltpu.CompilerParams(
             collective_id=1, has_side_effects=True, vmem_limit_bytes=48 * 2**20

time: 57.5 us -> 53.2 us (0.925)
  Pallas kernels: 53.4 us -> 49.4 us
    pallas_call x1, Pallas kernels: 53.4 us -> 49.4 us  [local(): pl.pallas_call(functools.partial(whole_kernel, sizes, half, entries, posi...]
where the time goes in v3:
time: 53.2 us
  Pallas kernels  49.4 us (93%)
  between operations  2.33 us (4%)
  local copies, waits for them, and re-layouts  1.5 us (3%)
    pallas_call x1, Pallas kernels, local(): pl.pallas_call(functools.partial(whole_kernel, sizes, half, entries, posi...  49.4 us
    unnamed x2, local copies, waits for them, and re-layouts  1.5 us

profile of v3, /device:TPU:0, one launch (start us, length us, event | category | flops | bytes accessed | tf_op | source)
XLA Modules:
  0.0 53.2 jit_solution(11029324257711898424)
XLA Ops:
  0.6 49.4 %shard_map.103 = (f32[2,2,4,32,128]{4,3,2,1,0:T(8,128)S(1)}, f32[512,256]{1,0:T(8,128)S(1)}, f32[1,1]{1,0:T(1,128)}) custom-call(s32[8]{0:T(128)} %bitcast.9, s32[8]{0:T(128)} %bitcast.10, bf16[16,256,128]{2,1,0:T(8,128)(2,1)} %phase_ref.1, bf16[16,256,128]{2,1,0:T(8,128)(2,1)} %absorb_ref.1, f32[2,256,256]{2,1,0:T(8,128)} %probe_in.1, ...), custom_call_target="tpu_custom_call" | custom-call | tf_op jit(solution)/shard_map/pallas_call | solution.py:530
  50.0 0.7 %copy.14 = f32[2,256,128]{2,1,0:T(8,128)} copy(f32[2,256,128]{2,1,0:T(8,128)S(1)} %bitcast.7) | data formatting | bytes 524288
  50.7 0.8 %copy.15 = f32[2,256,256]{2,1,0:T(8,128)} copy(f32[2,256,256]{2,1,0:T(8,128)S(1)} %bitcast.6) | data formatting | bytes 1048576

commit v4 on v3

--- a/solution.py
+++ b/solution.py
@@ -161,28 +161,51 @@
             "col", (at(1, block), at(2, block)), (at(1, block), at(0, block)), when, when, index=index
         ))
 
-    def along(share_at):
-        here = at(1, edge + share_at)
-        below = lax.rem(edge + beams + share_at, blocks)
-        above = lax.rem(edge + share_at + blocks - beams, blocks)
+    def rim_blocks(share_at):
+        return lax.rem(edge + beams + share_at, blocks), lax.rem(edge + share_at + blocks - beams, blocks)
+
+    def rim_here(share_at):
+        from_after = jnp.logical_and(row < rows_count - 1, share_at < edge)
+        from_before = jnp.logical_and(row > 0, share_at >= beams - edge)
+        return from_after, from_before
+
+    def along():
+        below, above = rim_blocks(beam)
         wait = net.sides(
-            "row", (here, at(1, below)), (here, at(1, above)), share_at < edge, share_at >= beams - edge,
+            "row", (at(1, own), at(1, below)), (at(1, own), at(1, above)), beam < edge, beam >= beams - edge,
             one_way=one_way,
         )
-        return wait, share_at, below, above
-
+        return wait, below, above
+
+    def around(peer, share_at):
+        waits = []
+        index = net.take()
+        for block, here, there in zip(rim_blocks(share_at), rim_here(share_at), rim_here(peer)):
+            one = net.copy({"beam": peer}, at(1, block), at(1, block), index)
+            pl.when(here)(one.start)
+            net.started.append(functools.partial(pl.when(here), one.wait_send))
+            waits.append(functools.partial(pl.when(there), one.wait_recv))
+            index = index if one_way or waits[1:] else net.take()
+        return lambda: [wait() for wait in waits]
+
+    def spread(share_at, below, above):
+        from_after, from_before = rim_here(share_at)
+        index = net.used if one_way and net.axes["col"][1] == 2 else None
+        across(below, from_after)
+        across(above, from_before, index)
+
+    wait_rim, below, above = along()
     gather = [net.send({"beam": peer}, at(1, own), at(1, own)) for peer in peers]
-    rims = [along(beam)]
     across(own)
+    wait_rim()
+    rims = [around(peer, beam) for peer in peers]
+    spread(beam, below, above)
     for peer, one in zip(peers, gather):
         one.wait_recv()
-        rims.append(along(peer))
         across(edge + peer)
-    for wait, share_at, below, above in rims:
+    for peer, wait in zip(peers, rims):
         wait()
-        index = net.used if one_way and net.axes["col"][1] == 2 else None
-        across(below, jnp.logical_and(row < rows_count - 1, share_at < edge))
-        across(above, jnp.logical_and(row > 0, share_at >= beams - edge), index)
+        spread(peer, *rim_blocks(peer))
     for wait in arrivals:
         wait()
     net.finish()
@@ -422,7 +445,8 @@
     mean_square = jnp.sum(total[0], keepdims=True) / entries
     factor = jnp.minimum(1.0, 0.5 / jnp.sqrt(mean_square + 1e-06))
     step_ref[...] = grads[...] * factor[None, None, None]
-    loss_ref[...] = jnp.sum(total[1], keepdims=True) * (1.0 / (positions * misfit_ref.shape[1] ** 2))
+    loss = jnp.sum(total[1], keepdims=True) * (1.0 / (positions * misfit_ref.shape[1] ** 2))
+    loss_ref[...] = jnp.broadcast_to(loss, loss_ref.shape)
     for one in col_copies:
         one.wait_recv()
     net.finish()
@@ -494,6 +518,19 @@
         side, strip, rims, folded, folded_in, grads,
         term_col, term_a, term_beam, term_b, term_row, small, small_in, small_all,
     )
+
+
+def close_kernel(step_in, probe_in, loss_in, step_ref, probe_ref, loss_ref, one, sems):
+    copies = [
+        pltpu.make_async_copy(src, dst, sems.at[k])
+        for k, (src, dst) in enumerate(((probe_in, probe_ref), (step_in, step_ref), (one, loss_ref)))
+    ]
+    copies[0].start()
+    copies[1].start()
+    one[...] = loss_in[:1, :1]
+    copies[2].start()
+    for copy in copies:
+        copy.wait()
 
 
 def pin(x):
@@ -529,7 +566,7 @@
     hbm = pl.BlockSpec(memory_space=pltpu.HBM)
     step, probe_gradient, loss = pl.pallas_call(
         functools.partial(whole_kernel, sizes, half, entries, positions),
-        out_shape=[jax.ShapeDtypeStruct(s, f32) for s in (grid, (2 * length, length), (1, 1))],
+        out_shape=[jax.ShapeDtypeStruct(s, f32) for s in (grid, (2 * length, length), (8, cols))],
         in_specs=[hbm] * 8,
         out_specs=vmem_specs(3),
         scratch_shapes=[
@@ -578,6 +615,14 @@
         pin(scan_rows.reshape(count)), pin(scan_cols.reshape(count)), pin(phase_volume), pin(absorb_volume), pin(probe),
         pin(amplitudes.reshape(count, length, length)), pin(left), pin(right),
     )
+    step, probe_gradient, loss = pl.pallas_call(
+        close_kernel,
+        out_shape=[jax.ShapeDtypeStruct(s, f32) for s in (grid, (2 * length, length), (1, 1))],
+        in_specs=vmem_specs(3),
+        out_specs=[hbm] * 3,
+        scratch_shapes=[vmem((1, 1), f32), pltpu.SemaphoreType.DMA((3,))],
+        compiler_params=pltpu.CompilerParams(vmem_limit_bytes=2**20),
+    )(step, probe_gradient, loss)
     return step.reshape(2, rows, cols), probe_gradient.reshape(probe.shape), loss.reshape(())
 
 

time: 53.2 us -> 49.8 us (0.936)
  between operations: 2.33 us -> 0.64 us
  local copies, waits for them, and re-layouts: 1.5 us -> 0 us
    unnamed x2 -> x0, local copies, waits for them, and re-layouts: 1.5 us -> none
    pallas_call x1, Pallas kernels: 49.4 us -> 48.1 us  [local(): pl.pallas_call(functools.partial(whole_kernel, sizes, half, entries, posi...]
    pallas_call x0 -> x1, Pallas kernels: none -> 0.91 us  [local(): pl.pallas_call(close_kernel, out_shape=[jax.ShapeDtypeStruct(s, f32) for...]
where the time goes in v4:
time: 49.8 us; the launch traced here: 49.6 us
  Pallas kernels  49 us (98%)
  between operations  0.64 us (1%)
    pallas_call x1, Pallas kernels, local(): pl.pallas_call(functools.partial(whole_kernel, sizes, half, entries, posi...  48.1 us

profile of v4, /device:TPU:0, one launch (start us, length us, event | category | flops | bytes accessed | tf_op | source)
XLA Modules:
  0.0 49.6 jit_solution(8750387412286865065)
XLA Ops:
  0.6 48.1 %shard_map.103 = (f32[2,2,4,32,128]{4,3,2,1,0:T(8,128)S(1)}, f32[512,256]{1,0:T(8,128)S(1)}, f32[8,128]{1,0:T(8,128)S(1)}) custom-call(s32[8]{0:T(128)} %bitcast.7, s32[8]{0:T(128)} %bitcast.8, bf16[16,256,128]{2,1,0:T(8,128)(2,1)} %phase_ref.1, bf16[16,256,128]{2,1,0:T(8,128)(2,1)} %absorb_ref.1, f32[2,256,256]{2,1,0:T(8,128)} %probe_in.1, ...), custom_call_target="tpu_custom_call" | custom-call | tf_op jit(solution)/shard_map/pallas_call | solution.py:567
  48.7 0.9 %shard_map.104 = (f32[2,2,4,32,128]{4,3,2,1,0:T(8,128)}, f32[512,256]{1,0:T(8,128)}, f32[1,1]{1,0:T(1,128)}) custom-call(f32[2,2,4,32,128]{4,3,2,1,0:T(8,128)S(1)} %get-tuple-element.9.step_in, f32[512,256]{1,0:T(8,128)S(1)} %get-tuple-element.10.probe_in, f32[8,128]{1,0:T(8,128)S(1)} %get-tuple-element.11.loss_in), custom_call_target="tpu_custom_call" | custom-call | tf_op jit(solution)/shard_map/pallas_call | solution.py:618

commit v5 on v4

--- a/solution.py
+++ b/solution.py
@@ -23,15 +23,9 @@
 
 
 def partners(me, count):
-    if count % 4 == 0:
-        high, low = me // 4 * 4 + me % 4 // 2 * 2, me % 2
-        flips = [(1, 1), (0, 1), (1, 0)]
-        near = []
-        for up, across in flips:
-            other = me // 4 * 4 + lax.rem(me % 4 // 2 + up, 2) * 2 + lax.rem(low + across, 2)
-            near.append(other)
-        if count == 4:
-            return near
+    if count == 4:
+        flips = ((1, 1), (0, 1), (1, 0))
+        return [lax.rem(me // 2 + up, 2) * 2 + lax.rem(me % 2 + across, 2) for up, across in flips]
     return [lax.rem(me + d, count) for d in range(1, count)]
 
 
@@ -144,6 +138,7 @@
             arrived()
         if i < beams - 1:
             scatter.append(net.send({"beam": peer}, part.at[i], slots.at[i]))
+    yield
     total = part[beams - 1]
     for i, one in enumerate(scatter):
         one.wait_recv()
@@ -288,9 +283,9 @@
                 moved[w % places, part, k, pl.ds(length + m, step), :] = jnp.where(first, after, before)
 
     def left(values, first, out, slot):
-        part = dot(first[...], values[slot])
-        out[slot, :, :length] = part[:length].astype(jnp.bfloat16)
-        out[slot, :, length:] = part[length:].astype(jnp.bfloat16)
+        for k in range(2):
+            part = dot(first[pl.ds(k * length, length), :], values[slot])
+            out[slot, :, k * length : (k + 1) * length] = part.astype(jnp.bfloat16)
 
     def halves(make, source, table, w, slot, cut):
         tall = length // cut
@@ -302,7 +297,23 @@
     def enters(w):
         if w < count:
             for m in range(steps):
-                enter(w, w % 2, m)
+                enter(w, w % slots, m)
+
+    def forth(w):
+        if w < count:
+            left(wave, left_ref, half, w % slots)
+
+    def judge(w):
+        if w < count:
+            halves(compare, half, right_ref, w, w % slots, 1)
+
+    def backs(w):
+        if w < count:
+            left(chi, right_ref, back, w % slots)
+
+    def leaves(w):
+        if 0 <= w < count:
+            halves(leave, back, left_ref, w, w % slots, 1)
 
     def place(pair, block, b, k):
         thin = canvas_ref.shape[4]
@@ -314,27 +325,27 @@
                 total = piece if total is None else total + piece
             canvas_ref[part, k, block, b] = total
 
-    pairs = count // 2
-    enters(0)
-    for p in range(pairs):
-        a, b = 2 * p, 2 * p + 1
-        left(wave, left_ref, half, 0)
-        if p:
-            halves(leave, back, left_ref, b - 2, 1, 2)
-        enters(b)
-        left(wave, left_ref, half, 1)
-        halves(compare, half, right_ref, a, 0, 2)
-        left(chi, right_ref, back, 0)
-        if p:
+    def settle(pair):
+        if 0 <= pair < pairs - 1:
             for block in range(canvas_ref.shape[2]):
                 for share in range(canvas_ref.shape[3]):
                     for k in range(spans):
-                        place(p - 1, block, share, k)
-        halves(compare, half, right_ref, b, 1, 2)
-        left(chi, right_ref, back, 1)
-        halves(leave, back, left_ref, a, 0, 2)
-        enters(a + 2)
-    halves(leave, back, left_ref, count - 1, 1, 2)
+                        place(pair, block, share, k)
+
+    slots = kept.shape[0]
+    pairs = count // 2
+    enters(0)
+    enters(1)
+    forth(0)
+    for w in range(count):
+        enters(w + 2)
+        judge(w)
+        forth(w + 1)
+        leaves(w - 1)
+        backs(w)
+        if w % 2 == 0:
+            settle(w // 2 - 1)
+    leaves(count - 1)
     return functools.partial(place, pairs - 1)
 
 
@@ -349,9 +360,11 @@
     col, cols_count = net.axes["col"]
     blocks = strip.shape[1]
     cols = strip.shape[4]
-    lines = term_b.shape[0]
+    thin = term_b.shape[1]
+    lines = rows_count * thin
     beam_peers, row_peers, col_peers = (net.others(axis) for axis in ("beam", "row", "col"))
     order = beam_peers + [beam]
+    row_order = row_peers[::2] + row_peers[1::2] + [row]
     wide = [{"beam": b, "row": r} for b in order for r in row_peers + [row]][:-1]
     rows_of = lambda c, b, n: pl.ds(pl.multiple_of((c * beams + b) * lines, lines), n * lines)
 
@@ -374,14 +387,20 @@
             place(block, p, 1)
     for one in term_copies:
         one.wait_recv()
-    term_beams = []
     for i, p in enumerate(order):
         total = term_ref[rows_of(col, p, 1), :]
         for k in range(cols_count - 1):
             total += term_col[k, pl.ds(pl.multiple_of(p * lines, lines), lines), :]
-        term_a[i] = total
-        if i < beams - 1:
-            term_beams.append(net.send({"beam": p}, term_a.at[i], term_beam.at[i]))
+        for r in range(rows_count):
+            term_a[i, r] = total[r * thin : (r + 1) * thin]
+    term_beams = []
+    for r in row_order:
+        index = net.take()
+        slots = term_beam.at[r]
+        for i, p in enumerate(beam_peers):
+            net.copy({"beam": p}, term_a.at[i, r], slots.at[i], index).start()
+        net.started.append(pltpu.make_async_copy(slots, slots, net.sends.at[index - net.base]).wait)
+        term_beams.append(pltpu.make_async_copy(slots, slots, net.recvs.at[index]).wait)
 
     along = []
     for i, p in enumerate(order):
@@ -393,7 +412,8 @@
             (strip.at[:, blocks - 1, p], rims.at[0, :, p]),
         ))
     grids = []
-    for i, p in enumerate(order):
+
+    def fold(i, p):
         along[i]()
         folded[i] = strip[:, 1 : blocks - 1, p]
         folded[i, :, 0] += rims[0, :, p]
@@ -401,12 +421,38 @@
         if i < beams - 1:
             grids.append(net.send({"beam": p}, folded.at[i], folded_in.at[i]))
 
-    total = term_a[beams - 1]
-    for i, one in enumerate(term_beams):
-        one.wait_recv()
-        total += term_beam[i]
-    term_b[...] = total
-    term_rows = [net.send({"row": r}, term_b, term_row.at[k]) for k, r in enumerate(row_peers)]
+    term_rows = []
+
+    def gather(k, r):
+        term_beams[k]()
+        total = term_a[beams - 1, r]
+        for i in range(beams - 1):
+            total += term_beam[r, i]
+        term_b[r] = total
+        if k < rows_count - 1:
+            term_rows.append(net.send({"row": r}, term_b.at[r], term_row.at[k]))
+
+    for i, p in enumerate(order):
+        fold(i, p)
+        if i < rows_count:
+            gather(i, row_order[i])
+    for k in range(beams, rows_count):
+        gather(k, row_order[k])
+
+    total = term_b[row]
+    for k, one in enumerate(term_rows):
+        one.wait_recv()
+        total += term_row[k]
+    probe_ref[col, beam, row] = total * (1.0 / positions)
+    piece = lambda r: probe_ref.at[col, beam, r]
+    term_rows = [net.send({"row": r}, piece(row), piece(row)) for r in row_peers]
+    around = [net.take() for _ in beam_peers]
+
+    def forward(r):
+        for p, index in zip(beam_peers, around):
+            net.copy({"beam": p}, piece(r), piece(r), index).start()
+
+    forward(row)
 
     total = folded[beams - 1]
     for i, one in enumerate(grids):
@@ -417,35 +463,35 @@
     misfit_sum = misfit_ref[:, :cols]
     for k in range(1, misfit_ref.shape[1] // cols):
         misfit_sum += misfit_ref[:, k * cols : (k + 1) * cols]
-    small[0] = jnp.sum((total * total).reshape(-1, 8, cols), axis=0)
-    small[1] = misfit_sum
+    small[:1] = jnp.sum((total * total).reshape(-1, cols), axis=0, keepdims=True)
+    small[1:] = jnp.sum(misfit_sum, axis=0, keepdims=True)
     small_wait = net.group(wide, small, small_in)
     mine = grads.at[:, :, beam]
     grid_copies = [net.send({"beam": p}, mine, mine) for p in beam_peers]
 
-    for one in term_rows:
-        one.wait_recv()
-    total = tree([term_row[k] for k in range(rows_count - 1)] + [term_b[...]])
-    probe_ref[rows_of(col, beam, 1), :] = total * (1.0 / positions)
-    share = lambda p: probe_ref.at[rows_of(col, p, 1), :]
-    term_copies = [net.send({"beam": p}, share(beam), share(beam)) for p in beam_peers]
+    for r, one in zip(row_peers, term_rows):
+        one.wait_recv()
+        forward(r)
+    share = lambda p: probe_ref.at[col, p]
+    for index in around:
+        net.started.append(pltpu.make_async_copy(share(beam), share(beam), net.sends.at[index - net.base]).wait)
     col_copies = [net.send({"col": c}, share(beam), share(beam)) for c in col_peers]
     small_wait()
     sums = [small_in[k] for k in range(beams * rows_count - 1)] + [small[...]]
     small_all[col] = tree([tree(sums[b * rows_count : (b + 1) * rows_count]) for b in range(beams)])
     smalls = [net.send({"col": c}, small_all.at[col], small_all.at[col]) for c in col_peers]
-    for p, one in zip(beam_peers, term_copies):
-        one.wait_recv()
+    for p, index in zip(beam_peers, around):
+        pltpu.make_async_copy(share(p), share(p), net.recvs.at[index]).wait()
         col_copies += [net.send({"col": c}, share(p), share(p)) for c in col_peers]
     for one in grid_copies + smalls:
         one.wait_recv()
     total = small_all[0]
     for k in range(1, cols_count):
         total += small_all[k]
-    mean_square = jnp.sum(total[0], keepdims=True) / entries
+    mean_square = jnp.sum(total[:1], keepdims=True) / entries
     factor = jnp.minimum(1.0, 0.5 / jnp.sqrt(mean_square + 1e-06))
     step_ref[...] = grads[...] * factor[None, None, None]
-    loss = jnp.sum(total[1], keepdims=True) * (1.0 / (positions * misfit_ref.shape[1] ** 2))
+    loss = jnp.sum(total[1:], keepdims=True) * (1.0 / (positions * misfit_ref.shape[1] ** 2))
     loss_ref[...] = jnp.broadcast_to(loss, loss_ref.shape)
     for one in col_copies:
         one.wait_recv()
@@ -477,8 +523,6 @@
             )
         )
     ]
-    for one in early:
-        one.start()
     misfit[...] = jnp.zeros_like(misfit)
 
     def empty(where):
@@ -506,6 +550,9 @@
     for k in range(moved.shape[0]):
         moved[k, :, :, :length, :] = blank
         moved[k, :, :, 2 * length :, :] = blank
+    next(stages)
+    for one in early:
+        one.start()
     next(stages)
     for one in early:
         one.wait()
@@ -555,18 +602,19 @@
     thin = half // beams
     chunk = 2 * length // cols_count
     lines = chunk // beams
+    pieces = (cols_count, beams, rows_count, lines // rows_count, length)
     grid = (2, blocks - 2, beams, thin, cols)
     entries = 2 * rows * cols * rows_count * cols_count
     ways = 1 if cols_count == 2 else 2
     one_way = 2 * half <= rows
     early = 2 * (beams - 1) + (1 if one_way else 2) * beams
     early += beams * (2 if one_way and ways == 1 else 3 * ways)
-    late = (cols_count - 1) * (2 + beams) + (ways + 2) * beams + 4 * (beams - 1) + rows_count
+    late = (cols_count - 1) * (2 + beams) + (ways + 2) * beams + 3 * (beams - 1) + 3 * rows_count - 1
     vmem = pltpu.VMEM
     hbm = pl.BlockSpec(memory_space=pltpu.HBM)
     step, probe_gradient, loss = pl.pallas_call(
         functools.partial(whole_kernel, sizes, half, entries, positions),
-        out_shape=[jax.ShapeDtypeStruct(s, f32) for s in (grid, (2 * length, length), (8, cols))],
+        out_shape=[jax.ShapeDtypeStruct(s, f32) for s in (grid, pieces, (8, cols))],
         in_specs=[hbm] * 8,
         out_specs=vmem_specs(3),
         scratch_shapes=[
@@ -580,11 +628,11 @@
             vmem((count, length, length), amplitudes.dtype),
             vmem(left.shape, bf16),
             vmem(right.shape, bf16),
-            vmem((2, 2, length, length), f32),
-            vmem((2, 2 * length, length), bf16),
-            vmem((2, length, 2 * length), bf16),
-            vmem((2, 2 * length, length), bf16),
-            vmem((2, length, 2 * length), bf16),
+            vmem((4, 2, length, length), f32),
+            vmem((4, 2 * length, length), bf16),
+            vmem((4, length, 2 * length), bf16),
+            vmem((4, 2 * length, length), bf16),
+            vmem((4, length, 2 * length), bf16),
             vmem((4, 2, 3, 3 * length, cols), f32),
             vmem((2, 3, blocks, beams, thin, cols), f32),
             vmem((2 * length, length), f32),
@@ -596,13 +644,13 @@
             vmem((beams - 1, 2, blocks - 2, thin, cols), f32),
             vmem(grid, f32),
             vmem((cols_count - 1, chunk, length), f32),
-            vmem((beams, lines, length), f32),
-            vmem((beams - 1, lines, length), f32),
-            vmem((lines, length), f32),
-            vmem((rows_count - 1, lines, length), f32),
-            vmem((2, 8, cols), f32),
-            vmem((beams * rows_count - 1, 2, 8, cols), f32),
-            vmem((cols_count, 2, 8, cols), f32),
+            vmem((beams,) + pieces[2:], f32),
+            vmem((rows_count, beams - 1) + pieces[3:], f32),
+            vmem(pieces[2:], f32),
+            vmem((rows_count - 1,) + pieces[3:], f32),
+            vmem((2, cols), f32),
+            vmem((beams * rows_count - 1, 2, cols), f32),
+            vmem((cols_count, 2, cols), f32),
             pltpu.SemaphoreType.DMA((beams,)),
             pltpu.SemaphoreType.DMA((6,)),
             pltpu.SemaphoreType.DMA((max(early, late),)),
@@ -617,7 +665,7 @@
     )
     step, probe_gradient, loss = pl.pallas_call(
         close_kernel,
-        out_shape=[jax.ShapeDtypeStruct(s, f32) for s in (grid, (2 * length, length), (1, 1))],
+        out_shape=[jax.ShapeDtypeStruct(s, f32) for s in (grid, pieces, (1, 1))],
         in_specs=vmem_specs(3),
         out_specs=[hbm] * 3,
         scratch_shapes=[vmem((1, 1), f32), pltpu.SemaphoreType.DMA((3,))],

time: 49.8 us -> 46.6 us (0.936)
  Pallas kernels: 49 us -> 45.8 us
    pallas_call x1, Pallas kernels: 48.1 us -> 44.9 us  [local(): pl.pallas_call(functools.partial(whole_kernel, sizes, half, entries, posi...]
where the time goes in v5:
time: 46.6 us; the launch traced here: 46.5 us
  Pallas kernels  45.8 us (98%)
  between operations  0.64 us (1%)
    pallas_call x1, Pallas kernels, local(): pl.pallas_call(functools.partial(whole_kernel, sizes, half, entries, posi...  44.9 us

profile of v5, /device:TPU:0, one launch (start us, length us, event | category | flops | bytes accessed | tf_op | source)
XLA Modules:
  0.0 46.5 jit_solution(4462810535980228603)
XLA Ops:
  0.6 44.9 %shard_map.103 = (f32[2,2,4,32,128]{4,3,2,1,0:T(8,128)S(1)}, f32[2,4,4,16,256]{4,3,2,1,0:T(8,128)S(1)}, f32[8,128]{1,0:T(8,128)S(1)}) custom-call(s32[8]{0:T(128)} %bitcast.7, s32[8]{0:T(128)} %bitcast.8, bf16[16,256,128]{2,1,0:T(8,128)(2,1)} %phase_ref.1, bf16[16,256,128]{2,1,0:T(8,128)(2,1)} %absorb_ref.1, f32[2,256,256]{2,1,0:T(8,128)} %probe_in.1, ...), custom_call_target="tpu_custom_call" | custom-call | tf_op jit(solution)/shard_map/pallas_call | solution.py:615
  45.6 0.9 %shard_map.104 = (f32[2,2,4,32,128]{4,3,2,1,0:T(8,128)}, f32[2,4,4,16,256]{4,3,2,1,0:T(8,128)}, f32[1,1]{1,0:T(1,128)}) custom-call(f32[2,2,4,32,128]{4,3,2,1,0:T(8,128)S(1)} %get-tuple-element.9.step_in, f32[2,4,4,16,256]{4,3,2,1,0:T(8,128)S(1)} %get-tuple-element.10.probe_in, f32[8,128]{1,0:T(8,128)S(1)} %get-tuple-element.11.loss_in), custom_call_target="tpu_custom_call" | custom-call | tf_op jit(solution)/shard_map/pallas_call | solution.py:666

commit v6 on v5

--- a/solution.py
+++ b/solution.py
@@ -64,12 +64,16 @@
         self.started.append(one.wait_send)
         return one
 
+    def joint(self, slots):
+        index = self.take()
+        self.started.append(pltpu.make_async_copy(slots, slots, self.sends.at[index - self.base]).wait)
+        return index, pltpu.make_async_copy(slots, slots, self.recvs.at[index]).wait
+
     def group(self, targets, src, slots):
-        index = self.take()
+        index, wait = self.joint(slots)
         for k, target in enumerate(targets):
             self.copy(target, src, slots.at[k], index).start()
-        self.started.append(pltpu.make_async_copy(slots, slots, self.sends.at[index - self.base]).wait)
-        return pltpu.make_async_copy(slots, slots, self.recvs.at[index]).wait
+        return wait
 
     def sides(self, axis, down, up, to_before=True, to_after=True, one_way=False, index=None):
         me, count = self.axes[axis]
@@ -126,7 +130,7 @@
             pltpu.make_async_copy(ref.at[:, here, :], volume.at[i, plane], load_sem.at[i]).start()
     arrived = net.greet()
     yield
-    scatter = []
+    joint, scatter_wait = net.joint(slots)
     for i, peer in enumerate(order):
         pltpu.make_async_copy(volume.at[i], volume.at[i], load_sem.at[i]).wait()
         for plane in range(2):
@@ -137,11 +141,11 @@
         if i == 0:
             arrived()
         if i < beams - 1:
-            scatter.append(net.send({"beam": peer}, part.at[i], slots.at[i]))
+            net.copy({"beam": peer}, part.at[i], slots.at[i], joint).start()
     yield
     total = part[beams - 1]
-    for i, one in enumerate(scatter):
-        one.wait_recv()
+    scatter_wait()
+    for i in range(beams - 1):
         total += slots[i]
     at = lambda side, block: out_ref.at[:, side, pl.ds(pl.multiple_of(block * share, share), share), :]
     damping = jnp.exp(-total[1])
@@ -208,7 +212,7 @@
 
 
 def windows(
-    rows_ref, cols_ref, trans_ref, probe_ref, amplitude_ref, left_ref, right_ref,
+    outer, rows_ref, cols_ref, trans_ref, probe_ref, amplitude_ref, left_ref, right_ref,
     canvas_ref, term_ref, misfit_ref, kept, wave, half, chi, back, moved,
 ):
     count, length = amplitude_ref.shape[:2]
@@ -329,7 +333,7 @@
         if 0 <= pair < pairs - 1:
             for block in range(canvas_ref.shape[2]):
                 for share in range(canvas_ref.shape[3]):
-                    for k in range(spans):
+                    for k in (1, *outer):
                         place(pair, block, share, k)
 
     slots = kept.shape[0]
@@ -350,7 +354,7 @@
 
 
 def combine(
-    net, place, entries, positions, canvas_ref, term_ref, misfit_ref,
+    net, outer, place, entries, positions, canvas_ref, term_ref, misfit_ref,
     step_ref, probe_ref, loss_ref,
     side, strip, rims, folded, folded_in, grads,
     term_col, term_a, term_beam, term_b, term_row, small, small_in, small_all,
@@ -375,8 +379,8 @@
     across = []
     for p in order:
         for block in range(blocks):
-            place(block, p, 0)
-            place(block, p, 2)
+            for k in outer:
+                place(block, p, k)
         across.append(net.sides(
             "col",
             (canvas_ref.at[:, 0, :, p], side.at[1, :, :, p]),
@@ -405,13 +409,16 @@
     along = []
     for i, p in enumerate(order):
         across[i]()
-        strip[:, :, p] = canvas_ref[:, 1, :, p] + side[0, :, :, p] + side[1, :, :, p]
+        if cols_count == 2:
+            strip[:, :, p] = canvas_ref[:, 1, :, p] + side[1 - col, :, :, p]
+        else:
+            strip[:, :, p] = canvas_ref[:, 1, :, p] + side[0, :, :, p] + side[1, :, :, p]
         along.append(net.sides(
             "row",
             (strip.at[:, 0, p], rims.at[1, :, p]),
             (strip.at[:, blocks - 1, p], rims.at[0, :, p]),
         ))
-    grids = []
+    grid_index, grid_wait = net.joint(folded_in)
 
     def fold(i, p):
         along[i]()
@@ -419,9 +426,9 @@
         folded[i, :, 0] += rims[0, :, p]
         folded[i, :, blocks - 3] += rims[1, :, p]
         if i < beams - 1:
-            grids.append(net.send({"beam": p}, folded.at[i], folded_in.at[i]))
-
-    term_rows = []
+            net.copy({"beam": p}, folded.at[i], folded_in.at[i], grid_index).start()
+
+    row_index, row_wait = net.joint(term_row)
 
     def gather(k, r):
         term_beams[k]()
@@ -430,7 +437,7 @@
             total += term_beam[r, i]
         term_b[r] = total
         if k < rows_count - 1:
-            term_rows.append(net.send({"row": r}, term_b.at[r], term_row.at[k]))
+            net.copy({"row": r}, term_b.at[r], term_row.at[k], row_index).start()
 
     for i, p in enumerate(order):
         fold(i, p)
@@ -440,8 +447,8 @@
         gather(k, row_order[k])
 
     total = term_b[row]
-    for k, one in enumerate(term_rows):
-        one.wait_recv()
+    row_wait()
+    for k in range(rows_count - 1):
         total += term_row[k]
     probe_ref[col, beam, row] = total * (1.0 / positions)
     piece = lambda r: probe_ref.at[col, beam, r]
@@ -455,8 +462,8 @@
     forward(row)
 
     total = folded[beams - 1]
-    for i, one in enumerate(grids):
-        one.wait_recv()
+    grid_wait()
+    for i in range(beams - 1):
         total += folded_in[i]
     grads[0, :, beam] = total[0]
     grads[1, :, beam] = -total[1]
@@ -556,12 +563,13 @@
     next(stages)
     for one in early:
         one.wait()
+    outer = (2 - 2 * col,) if cols_count == 2 else (0, 2)
     place = windows(
-        rows_ref, cols_ref, trans, probe, amplitude, left, right,
+        outer, rows_ref, cols_ref, trans, probe, amplitude, left, right,
         canvas, term, misfit, kept, wave, half, chi, back, moved,
     )
     combine(
-        net, place, entries, positions, canvas, term, misfit, step_ref, probe_out, loss_ref,
+        net, outer, place, entries, positions, canvas, term, misfit, step_ref, probe_out, loss_ref,
         side, strip, rims, folded, folded_in, grads,
         term_col, term_a, term_beam, term_b, term_row, small, small_in, small_all,
     )
@@ -607,9 +615,9 @@
     entries = 2 * rows * cols * rows_count * cols_count
     ways = 1 if cols_count == 2 else 2
     one_way = 2 * half <= rows
-    early = 2 * (beams - 1) + (1 if one_way else 2) * beams
+    early = beams + (1 if one_way else 2) * beams
     early += beams * (2 if one_way and ways == 1 else 3 * ways)
-    late = (cols_count - 1) * (2 + beams) + (ways + 2) * beams + 3 * (beams - 1) + 3 * rows_count - 1
+    late = (cols_count - 1) * (2 + beams) + (ways + 2) * beams + 2 * beams + 2 * rows_count
     vmem = pltpu.VMEM
     hbm = pl.BlockSpec(memory_space=pltpu.HBM)
     step, probe_gradient, loss = pl.pallas_call(

time: 46.6 us -> 46.3 us (level)
  no operation moved by 1% of the time
where the time goes in v6:
time: 46.3 us; the launch traced here: 46.2 us
  Pallas kernels  45.5 us (98%)
  between operations  0.64 us (1%)
    pallas_call x1, Pallas kernels, local(): pl.pallas_call(functools.partial(whole_kernel, sizes, half, entries, posi...  44.6 us

profile of v6, /device:TPU:0, one launch (start us, length us, event | category | flops | bytes accessed | tf_op | source)
XLA Modules:
  0.0 46.2 jit_solution(2425741547575180206)
XLA Ops:
  0.6 44.6 %shard_map.103 = (f32[2,2,4,32,128]{4,3,2,1,0:T(8,128)S(1)}, f32[2,4,4,16,256]{4,3,2,1,0:T(8,128)S(1)}, f32[8,128]{1,0:T(8,128)S(1)}) custom-call(s32[8]{0:T(128)} %bitcast.7, s32[8]{0:T(128)} %bitcast.8, bf16[16,256,128]{2,1,0:T(8,128)(2,1)} %phase_ref.1, bf16[16,256,128]{2,1,0:T(8,128)(2,1)} %absorb_ref.1, f32[2,256,256]{2,1,0:T(8,128)} %probe_in.1, ...), custom_call_target="tpu_custom_call" | custom-call | tf_op jit(solution)/shard_map/pallas_call | solution.py:623
  45.3 0.9 %shard_map.104 = (f32[2,2,4,32,128]{4,3,2,1,0:T(8,128)}, f32[2,4,4,16,256]{4,3,2,1,0:T(8,128)}, f32[1,1]{1,0:T(1,128)}) custom-call(f32[2,2,4,32,128]{4,3,2,1,0:T(8,128)S(1)} %get-tuple-element.9.step_in, f32[2,4,4,16,256]{4,3,2,1,0:T(8,128)S(1)} %get-tuple-element.10.probe_in, f32[8,128]{1,0:T(8,128)S(1)} %get-tuple-element.11.loss_in), custom_call_target="tpu_custom_call" | custom-call | tf_op jit(solution)/shard_map/pallas_call | solution.py:674
